TPU v7x, 32 devices: a whole 2x2x4 slice. The times are simulated.
32 devices in a mesh: tile: 2 (over y), beam: 4 (over z), bl: 2 (over x), pol: 2 (over core).
Axes of the slice: x: 2, y: 2, z: 4, core: 2. Of those that a mesh axis runs over, the one named last changes fastest.
Arguments:
- sky_model: bfloat16 [4096, 4096], P(('tile', 'bl', 'pol'), 'beam'), parts along dimension 0, may hold values from -6 to 6
- beam_pattern: bfloat16 [8, 2048, 2048], P(('tile', 'beam'), ('bl', 'pol')), parts along dimension 0, may hold values from 0.099609375 to 1
- kernels: bfloat16 [8, 256, 128, 128], P(('tile', 'beam'), ('bl', 'pol')), parts along dimension 0, may hold values from -0.5 to 0.5
- observed: float32 [8, 256, 2, 128], P(('tile', 'beam'), ('bl', 'pol')), parts along dimension 0, may hold values from -6 to 6
- tile_owner: int32 [8, 256, 1], P(('tile', 'beam'), ('bl', 'pol')), parts along dimension 0, may hold values from 0 to 3; in each aligned block of 64 rows (0 to 63, 64 to 127, ..., all dimensions but the last counted through in order) at most 32 rows name the same one
- tile_local: int32 [8, 256], P(('tile', 'beam'), ('bl', 'pol')), parts along dimension 0, may hold values from 0 to 4095
- vis_count: int32 [8, 256], P(('tile', 'beam'), ('bl', 'pol')), parts along dimension 0, may hold values from 1 to 128
Outputs:
- residual_vis: float32 [8, 256, 2, 128], P(('tile', 'beam'), ('bl', 'pol')), parts along dimension 0
- dirty_grid: float32 [8, 16384, 2, 128], P(('tile', 'beam'), ('bl', 'pol')), parts along dimension 0
There are 2 independent parts, one for each index of `tile`. A program takes and returns all parts, laid end to end along the dimension named above; each array names one. Nothing has to cross between parts.
Inputs may be any that keep to these rules, and one draw needn't show every extreme that they name: `tile_owner`: among the 64 visibility tiles of one device, at most 32 name the same owner, and in some blocks one owner is named exactly 32 times.
All inputs are finite; a program needn't handle non-finite values.
Results may differ from a plain program's by a relative error of at most 0.0055.
Values may be sent and summed in bfloat16 or wider, within the bound.
A program may use at most 64 MiB of HBM per device.

v0:
```python
import functools
import math

import jax
import jax.numpy as jnp
import numpy as np
from jax import lax
from jax.experimental import pallas as pl
from jax.experimental.pallas import tpu as pltpu
from jax.sharding import PartitionSpec as P

MESH = pl.DeviceIdType.MESH
RADIX = 8
WIDE = 16
VMEM = pl.BlockSpec(memory_space=pltpu.VMEM)
HBM = pl.BlockSpec(memory_space=pltpu.HBM)
NT = (((1,), (1,)), ((), ()))
NN = (((1,), (0,)), ((), ()))


def wave(rows, cols, period, factor):
    angle = (np.outer(rows, cols) % period) * (2.0 * math.pi / period)
    return np.cos(angle) * factor, np.sin(angle) * factor


def first_tables(grid):
    span = grid // RADIX
    blocks = grid // 2 // RADIX
    cols = np.arange(span)

    def of(i):
        return wave(RADIX * np.arange(blocks) + i, cols, grid, grid**-0.5)

    real = []
    for i in (0, RADIX // 2):
        cos, sin = of(i)
        real.append(np.concatenate([cos, -sin], 0))
    pairs = []
    for i in range(1, RADIX // 2):
        cos, sin = of(i)
        cos_m, sin_m = of(RADIX - i)
        pairs.append(
            np.concatenate(
                [
                    np.concatenate([cos, sin], 1),
                    np.concatenate([-sin, cos], 1),
                    np.concatenate([cos_m, -sin_m], 1),
                    np.concatenate([-sin_m, -cos_m], 1),
                ],
                0,
            )
        )
    return np.stack(real).astype(jnp.bfloat16), np.stack(pairs).astype(jnp.bfloat16)


def second_tables(grid):
    period = grid // WIDE
    phase = np.stack(wave(np.arange(period), np.arange(period), period, 1.0), 1).astype(np.float32)
    cos, sin = wave(np.arange(grid), np.arange(WIDE), grid, grid**-0.5)
    cos, sin = np.tile(cos, (1, RADIX)), np.tile(sin, (1, RADIX))
    cos, sin = cos.reshape(-1, period, cos.shape[1]), sin.reshape(-1, period, sin.shape[1])
    table = np.concatenate([np.concatenate([cos, -sin], 2), np.concatenate([sin, cos], 2)], 1)
    return phase, table.astype(jnp.bfloat16)


def group_index():
    return lax.axis_index("bl") * lax.axis_size("pol") + lax.axis_index("pol")


def group_device(index):
    pol = lax.axis_size("pol")
    return {"bl": lax.div(index, pol), "pol": lax.rem(index, pol)}


def transform_rows(beams, at, pattern, strip, low, high, real_table, pair_table, g_real, g_pair, re, im):
    span = pattern.shape[1] // RADIX
    width = low.shape[1]
    beam = lax.axis_index("beam")
    step = 32
    root = math.sqrt(0.5)

    def fold(index, carry):
        src = pl.ds(pl.multiple_of(at + index * step, step), step)
        dst = pl.ds(pl.multiple_of(index * step, step), step)
        left = jnp.where(beam > 0, low[src, :], jnp.zeros((step, width), low.dtype))
        right = jnp.where(beam < beams - 1, high[src, :], jnp.zeros((step, width), high.dtype))
        window = jnp.concatenate([left, strip[src, :], right], axis=1)
        parts = []
        for a in range(RADIX):
            cut = slice(a * span, (a + 1) * span)
            weighted = pattern[src, cut].astype(jnp.float32) * window[:, cut].astype(jnp.float32)
            parts.append(weighted.astype(jnp.bfloat16).astype(jnp.float32))
        s = [parts[a] + parts[a + 4] for a in range(4)]
        d = [parts[a] - parts[a + 4] for a in range(4)]
        even, odd = s[0] + s[2], s[1] + s[3]
        near, far = root * (d[1] - d[3]), root * (d[1] + d[3])

        def put(ref, lead, off, value):
            ref[lead, dst, off : off + span] = value.astype(jnp.bfloat16)

        put(g_real, 0, 0, even + odd)
        put(g_real, 1, 0, even - odd)
        put(g_pair, 0, 0, d[0] + near)
        put(g_pair, 0, span, -(d[2] + far))
        put(g_pair, 1, 0, s[0] - s[2])
        put(g_pair, 1, span, s[3] - s[1])
        put(g_pair, 2, 0, d[0] - near)
        put(g_pair, 2, span, d[2] - far)
        return carry

    lax.fori_loop(0, g_real.shape[1] // step, fold, 0)
    blocks = re.shape[0]
    re = re.reshape(blocks * RADIX, re.shape[2])
    im = im.reshape(blocks * RADIX, im.shape[2])
    for k, i in enumerate((0, RADIX // 2)):
        out = lax.dot_general(real_table[k], g_real[k], NT, preferred_element_type=jnp.float32)
        re[pl.ds(i, blocks, stride=RADIX), :] = out[:blocks]
        im[pl.ds(i, blocks, stride=RADIX), :] = out[blocks:]
    for k in range(RADIX // 2 - 1):
        out = lax.dot_general(pair_table[k], g_pair[k], NT, preferred_element_type=jnp.float32)
        for n, (ref, i) in enumerate(((re, k + 1), (im, k + 1), (re, RADIX - 1 - k), (im, RADIX - 1 - k))):
            ref[pl.ds(i, blocks, stride=RADIX), :] = out[n * blocks : (n + 1) * blocks]


def asked_tiles(asker, codes, phase, weights, re, im, turned):
    period = phase.shape[2]
    vis = turned.shape[0] // RADIX
    cells = RADIX * WIDE
    own = lax.broadcasted_iota(jnp.int32, (RADIX, 2 * cells), 0)
    column = lax.broadcasted_iota(jnp.int32, (RADIX, 2 * cells), 1)
    keep = own == (column % cells) // WIDE

    def one(r):
        tile = codes[asker, 0, r]
        turn = phase[jnp.bitwise_and(tile, period - 1)]
        cos, sin = turn[0:1], turn[1:2]
        up = lax.shift_right_logical(tile, period.bit_length() - 1)
        x, y = re[up], im[up]
        return jnp.concatenate([x * cos + y * sin, y * cos - x * sin], axis=1)

    def turn_pair(p, carry):
        both = jnp.concatenate([one(2 * p), one(2 * p + 1)], axis=0)
        turned[pl.ds(pl.multiple_of(p * 2 * RADIX, 2 * RADIX), 2 * RADIX), :] = both.astype(jnp.bfloat16)
        return carry

    lax.fori_loop(0, vis // 2, turn_pair, 0, unroll=8)
    cells_of = lax.dot_general(turned[...], weights, NN, preferred_element_type=jnp.float32)
    picked = jnp.where(keep[None], cells_of.reshape(vis, RADIX, 2 * cells), 0.0)
    return jnp.sum(picked, axis=1)


def predict_kernel(
    group, beams, tiles_dev,
    sky, pattern_in, kernels_in, observed, owner, place, counts, real_in, pair_in, phase_in, table_in,
    residual, shared, codes,
    strip, low, high, pattern, kernels, real_table, pair_table, phase, table, code, codes_s,
    g_real, g_pair, re, im, turned, total, part, came, given, wide, narrow,
    local, halo_send, halo_recv, code_send, code_recv, part_send, part_recv, share_send, share_recv,
):
    beam = lax.axis_index("beam")
    me = group_index()
    vis, cells = kernels.shape[0], kernels.shape[1]
    width = low.shape[1]
    period = phase.shape[2]
    chunks = pattern.shape[0] // period

    loads = []
    for n, (src, dst) in enumerate((
        (pattern_in, pattern), (sky, strip), (real_in, real_table), (pair_in, pair_table), (phase_in, phase),
        (table_in.at[pl.ds(me * chunks, chunks)], table), (kernels_in, kernels),
    )):
        load = pltpu.make_async_copy(src, dst, local.at[n])
        load.start()
        loads.append(load)

    named = jnp.broadcast_to(owner[...] * tiles_dev + place[...], (code.shape[0], vis))
    for n in range(code.shape[1] // vis):
        code[:, n * vis : (n + 1) * vis] = named

    barrier = pltpu.get_barrier_semaphore()
    has_next, has_last = beam < beams - 1, beam > 0

    def greet(device):
        pl.semaphore_signal(barrier, inc=1, device_id=device, device_id_type=MESH)

    for step in range(1, group):
        greet(group_device(lax.rem(me + step, group)))

    @pl.when(has_next)
    def _():
        greet({"beam": beam + 1})

    @pl.when(has_last)
    def _():
        greet({"beam": beam - 1})

    edges = jnp.where(beam < beams - 1, 1, 0) + jnp.where(beam > 0, 1, 0)
    pl.semaphore_wait(barrier, group - 1 + edges)

    def halo(side, k):
        rows = pl.ds(pl.multiple_of(k * period, period), period)
        first = 0 if side else sky.shape[1] - width
        return pltpu.make_async_remote_copy(
            src_ref=sky.at[rows, pl.ds(first, width)], dst_ref=(high if side else low).at[rows, :],
            send_sem=halo_send.at[side, k], recv_sem=halo_recv.at[side, k],
            device_id={"beam": beam - 1 if side else beam + 1}, device_id_type=MESH,
        )

    def to_peer(step, source, target, send, recv):
        return pltpu.make_async_remote_copy(
            src_ref=source, dst_ref=target,
            send_sem=send.at[step - 1], recv_sem=recv.at[step - 1],
            device_id=group_device(lax.rem(me + step, group)), device_id_type=MESH,
        )

    @pl.when(has_next)
    def _():
        for k in range(chunks):
            halo(0, k).start()

    @pl.when(has_last)
    def _():
        for k in range(chunks):
            halo(1, k).start()

    named_copies = [to_peer(step, code, codes.at[me], code_send, code_recv) for step in range(1, group)]
    for copy in named_copies:
        copy.start()
    codes[me] = code[...]
    total[...] = jnp.zeros_like(total)
    wide[...] = jnp.zeros_like(wide)
    for copy in named_copies:
        copy.wait()
    to_scalar = pltpu.make_async_copy(codes, codes_s, local.at[len(loads)])
    to_scalar.start()
    to_scalar.wait()
    for load in loads[:-1]:
        load.wait()

    def of_chunk(k, carry):
        @pl.when(has_last)
        def _():
            halo(0, k).wait_recv()

        @pl.when(has_next)
        def _():
            halo(1, k).wait_recv()

        transform_rows(
            beams, k * period, pattern, strip, low, high, real_table, pair_table, g_real, g_pair, re, im
        )

        def of_asker(step, inner):
            asker = lax.rem(me + step, group)
            rows = pl.ds(pl.multiple_of(asker * vis, vis), vis)
            total[rows, :] += asked_tiles(asker, codes_s, phase, table[k], re, im, turned)

            @pl.when((k == chunks - 1) & (step < group))
            def _():
                part[rows, :] = total[rows, :].astype(part.dtype)
                to_peer(step, part.at[rows, :], came.at[me], part_send, part_recv).start()

            return inner

        lax.fori_loop(1, group + 1, of_asker, 0)
        return carry

    lax.fori_loop(0, chunks, of_chunk, 0)

    own = lax.broadcasted_iota(jnp.int32, (vis, vis), 0) == lax.broadcasted_iota(jnp.int32, (vis, vis), 1)
    count = jnp.sum(jnp.where(own, counts[...].astype(jnp.float32), 0.0), axis=1, keepdims=True)
    mask = lax.broadcasted_iota(jnp.int32, (vis, cells), 1).astype(jnp.float32) < count
    mine = total[pl.ds(pl.multiple_of(me * vis, vis), vis), :]
    loads[-1].wait()
    for step in range(1, group):
        rows = pl.ds(pl.multiple_of(lax.rem(me + step, group) * vis, vis), vis)
        to_peer(step, part.at[rows, :], came.at[me], part_send, part_recv).wait()
    for step in range(1, group):
        mine = mine + came[lax.rem(me + step, group)].astype(jnp.float32)
    for c in range(2):
        wide[pl.ds(c, vis, stride=RADIX), :] = mine[:, c * cells : (c + 1) * cells]

    def apply(dims):
        def of_tile(r, carry):
            at = pl.ds(pl.multiple_of(r * RADIX, RADIX), RADIX)
            narrow[at, :] = lax.dot_general(
                wide[at, :].astype(jnp.bfloat16), kernels[r], dims, preferred_element_type=jnp.float32
            )
            return carry

        lax.fori_loop(0, vis, of_tile, 0, unroll=16)

    apply(NT)
    for c in range(2):
        seen = observed[pl.ds(c, vis, stride=2), :]
        left = jnp.where(mask, seen - narrow[pl.ds(c, vis, stride=RADIX), :], 0.0)
        residual[pl.ds(c, vis, stride=2), :] = left
        wide[pl.ds(c, vis, stride=RADIX), :] = left
    apply(NN)
    for c in range(2):
        given[:, c * cells : (c + 1) * cells] = narrow[pl.ds(c, vis, stride=RADIX), :].astype(given.dtype)
    given_copies = [to_peer(step, given, shared.at[me], share_send, share_recv) for step in range(1, group)]
    for copy in given_copies:
        copy.start()
    shared[me] = given[...]
    for copy in given_copies:
        copy.wait()

    @pl.when(has_next)
    def _():
        for k in range(chunks):
            halo(0, k).wait_send()

    @pl.when(has_last)
    def _():
        for k in range(chunks):
            halo(1, k).wait_send()


def dirty_kernel(vis, codes, terms, left, dirty, residual, held, sems):
    blocks, rows, cells = held.shape
    rows = rows // 2
    group, _, lanes = codes.shape
    start = group_index() * rows * blocks
    residual[...] = left[...]
    each = lanes // vis
    lane = lax.broadcasted_iota(jnp.int32, (1, lanes), 1)
    keys = []
    for first in range(0, group, each):
        key = codes[first, 0:1, :]
        for n in range(1, each):
            key = jnp.where(lane < n * vis, key, codes[first + n, 0:1, :])
        keys.append(key)
    key = jnp.concatenate(keys, axis=1) - start
    tile = lax.broadcasted_iota(jnp.int32, (rows, key.shape[1]), 0)
    copies = []
    for block in range(blocks):
        onehot = jnp.where(tile == key - block * rows, 1.0, 0.0).astype(jnp.bfloat16)
        out = lax.dot_general(onehot, terms[...], NN, preferred_element_type=jnp.float32)
        for c in range(2):
            held[block, pl.ds(c, rows, stride=2), :] = out[:, c * cells : (c + 1) * cells]
        copy = pltpu.make_async_copy(
            held.at[block], dirty.at[pl.ds(block * rows * 2, rows * 2), :], sems.at[block]
        )
        copy.start()
        copies.append(copy)
    for copy in copies:
        copy.wait()


def on_device(sky_model, beam_pattern, kernels, observed, tile_owner, tile_local, vis_count):
    group = lax.axis_size(("bl", "pol"))
    beams = lax.axis_size("beam")
    rows, grid = beam_pattern.shape[1:]
    strip = sky_model.shape[1]
    halo = (grid - strip) // 2
    vis, cells = kernels.shape[1], kernels.shape[3]
    tiles_dev = (grid // 2 // RADIX) * (grid // WIDE) // group
    lanes = 128
    f32, bf16 = jnp.float32, jnp.bfloat16
    real_table, pair_table = first_tables(grid)
    phase, table = second_tables(grid)
    span, period = grid // RADIX, grid // WIDE
    chunks = rows // period
    dma = pltpu.SemaphoreType.DMA

    residual, shared, codes = pl.pallas_call(
        functools.partial(predict_kernel, group, beams, tiles_dev),
        out_shape=(
            jax.ShapeDtypeStruct((vis * 2, cells), f32),
            jax.ShapeDtypeStruct((group, vis, 2 * cells), bf16),
            jax.ShapeDtypeStruct((group, 8, lanes), jnp.int32),
        ),
        in_specs=[HBM, HBM, HBM, VMEM, VMEM, VMEM, VMEM, HBM, HBM, HBM, HBM],
        out_specs=(VMEM, VMEM, VMEM),
        scratch_shapes=[
            pltpu.VMEM((rows, strip), bf16),
            pltpu.VMEM((rows, halo), bf16),
            pltpu.VMEM((rows, halo), bf16),
            pltpu.VMEM((rows, grid), bf16),
            pltpu.VMEM((vis, cells, cells), bf16),
            pltpu.VMEM(real_table.shape, bf16),
            pltpu.VMEM(pair_table.shape, bf16),
            pltpu.VMEM(phase.shape, f32),
            pltpu.VMEM((chunks, *table.shape[1:]), bf16),
            pltpu.VMEM((8, lanes), jnp.int32),
            pltpu.SMEM((group, 8, lanes), jnp.int32),
            pltpu.VMEM((2, period, span), bf16),
            pltpu.VMEM((RADIX // 2 - 1, period, 2 * span), bf16),
            pltpu.VMEM((grid // 2 // RADIX, RADIX, period), f32),
            pltpu.VMEM((grid // 2 // RADIX, RADIX, period), f32),
            pltpu.VMEM((vis * RADIX, 2 * period), bf16),
            pltpu.VMEM((group * vis, 2 * cells), f32),
            pltpu.VMEM((group * vis, 2 * cells), bf16),
            pltpu.VMEM((group, vis, 2 * cells), bf16),
            pltpu.VMEM((vis, 2 * cells), bf16),
            pltpu.VMEM((vis * RADIX, cells), f32),
            pltpu.VMEM((vis * RADIX, cells), f32),
            dma((8,)),
            dma((2, chunks)), dma((2, chunks)),
            dma((group - 1,)), dma((group - 1,)),
            dma((group - 1,)), dma((group - 1,)),
            dma((group - 1,)), dma((group - 1,)),
        ],
        compiler_params=pltpu.CompilerParams(
            collective_id=0, has_side_effects=True, vmem_limit_bytes=60 * 1024 * 1024
        ),
        name="predict",
    )(
        sky_model, beam_pattern[0], kernels[0], observed.reshape(vis * 2, cells),
        tile_owner.reshape(1, vis), tile_local, vis_count,
        jnp.asarray(real_table), jnp.asarray(pair_table), jnp.asarray(phase), jnp.asarray(table),
    )

    blocks = 8
    dirty, residual = pl.pallas_call(
        functools.partial(dirty_kernel, vis),
        out_shape=(
            jax.ShapeDtypeStruct((tiles_dev * 2, cells), f32),
            jax.ShapeDtypeStruct((vis * 2, cells), f32),
        ),
        in_specs=[VMEM, VMEM, VMEM],
        out_specs=(HBM, VMEM),
        scratch_shapes=[pltpu.VMEM((blocks, tiles_dev * 2 // blocks, cells), f32), dma((blocks,))],
        name="dirty",
    )(codes, shared.reshape(group * vis, 2 * cells), residual)
    return (
        residual.reshape(1, vis, 2, cells),
        dirty.reshape(1, tiles_dev, 2, cells),
    )


def solution(mesh):
    placed = (
        P(("tile", "bl", "pol"), "beam"),
        P(("tile", "beam"), ("bl", "pol"), None),
        P(("tile", "beam"), ("bl", "pol"), None, None),
        P(("tile", "beam"), ("bl", "pol"), None, None),
        P(("tile", "beam"), ("bl", "pol"), None),
        P(("tile", "beam"), ("bl", "pol")),
        P(("tile", "beam"), ("bl", "pol")),
    )
    return jax.shard_map(
        on_device,
        mesh=mesh,
        in_specs=placed,
        out_specs=(
            P(("tile", "beam"), ("bl", "pol"), None, None),
            P(("tile", "beam"), ("bl", "pol"), None, None),
        ),
        check_vma=False,
    )
```

profile of v0, /device:TPU:0, one launch (start us, length us, event | category | flops | bytes accessed | tf_op | source)
XLA Modules:
  0.0 37.1 jit_solution(9693363317926575507)
XLA Ops:
  0.6 32.5 %predict.1 = (f32[128,128]{1,0:T(8,128)}, bf16[4,64,256]{2,1,0:T(8,128)(2,1)}, s32[4,8,128]{2,1,0:T(8,128)}) custom-call(bf16[512,1024]{1,0:T(8,128)(2,1)} %sky.1, bf16[512,2048]{1,0:T(8,128)(2,1)} %bitcast.7, bf16[64,128,128]{2,1,0:T(8,128)(2,1)} %bitcast.8, f32[128,128]{1,0:T(8,128)} %bitcast.10, s32[1,64]{1,0:T(1,128)} %bitcast.11, s32[1,64]{1,0:T(1,128)} %place.1, ...), custom_call_target="tpu_custom_call" | custom-call | tf_op jit(solution)/shard_map/predict/pallas_call | solution.py:367
  33.1 3.9 %dirty.1 = (f32[8192,128]{1,0:T(8,128)}, f32[128,128]{1,0:T(8,128)}) custom-call(s32[4,8,128]{2,1,0:T(8,128)} %get-tuple-element.7.codes, bf16[256,256]{1,0:T(8,128)(2,1)} %bitcast.9, f32[128,128]{1,0:T(8,128)} %get-tuple-element.9.left), custom_call_target="tpu_custom_call" | custom-call | tf_op jit(solution)/shard_map/dirty/pallas_call | solution.py:416
where the time goes:
time: 37.2 us; the launch traced here: 37.1 us
  Pallas kernels  36.4 us (98%)
  between operations  0.64 us (2%)
    pallas_call x1, Pallas kernels, on_device(): pl.pallas_call(functools.partial(predict_kernel, group, beams, tiles_dev)...  32.5 us
    pallas_call x1, Pallas kernels, on_device(): pl.pallas_call(functools.partial(dirty_kernel, vis), out_shape=(jax.Shape...  3.92 us

commit v1 on v0

v1 whole, which is shorter than its diff:
```python
import functools
import math

import jax
import jax.numpy as jnp
import numpy as np
from jax import lax
from jax.experimental import pallas as pl
from jax.experimental.pallas import tpu as pltpu
from jax.sharding import PartitionSpec as P

MESH = pl.DeviceIdType.MESH
RADIX = 8
WIDE = 16
scope = jax.named_scope
VMEM = pl.BlockSpec(memory_space=pltpu.VMEM)
HBM = pl.BlockSpec(memory_space=pltpu.HBM)
NT = (((1,), (1,)), ((), ()))
NN = (((1,), (0,)), ((), ()))


def wave(rows, cols, period, factor):
    angle = (np.outer(rows, cols) % period) * (2.0 * math.pi / period)
    return np.cos(angle) * factor, np.sin(angle) * factor


def first_tables(grid):
    span = grid // RADIX
    blocks = grid // 2 // RADIX
    cols = np.arange(span)

    def of(i):
        return wave(RADIX * np.arange(blocks) + i, cols, grid, grid**-0.5)

    real = []
    for i in (0, RADIX // 2):
        cos, sin = of(i)
        real.append(np.concatenate([cos, -sin], 0))
    pairs = []
    for i in range(1, RADIX // 2):
        cos, sin = of(i)
        cos_m, sin_m = of(RADIX - i)
        pairs.append(
            np.concatenate(
                [
                    np.concatenate([cos, sin], 1),
                    np.concatenate([-sin, cos], 1),
                    np.concatenate([cos_m, -sin_m], 1),
                    np.concatenate([-sin_m, -cos_m], 1),
                ],
                0,
            )
        )
    return np.stack(real).astype(jnp.bfloat16), np.stack(pairs).astype(jnp.bfloat16)


def second_tables(grid):
    period = grid // WIDE
    phase = np.stack(wave(np.arange(period), np.arange(period), period, 1.0), 1)
    cos, sin = wave(np.arange(period), np.arange(WIDE), grid, grid**-0.5)
    fine = np.stack([np.tile(cos, (1, RADIX)), np.tile(sin, (1, RADIX))])
    cos, sin = wave(np.arange(WIDE), np.arange(WIDE), WIDE, 1.0)
    coarse = np.stack([np.tile(cos, (1, RADIX)), np.tile(sin, (1, RADIX))], 1)
    return phase.astype(np.float32), fine.astype(np.float32), coarse.astype(np.float32)


def group_index():
    return lax.axis_index("bl") * lax.axis_size("pol") + lax.axis_index("pol")


def chip_peer(turn, core):
    chips, cores = lax.axis_size("bl"), lax.axis_size("pol")
    chip = lax.rem(lax.axis_index("bl") + turn, chips)
    return chip, lax.rem(lax.axis_index("pol") + core, cores)


def transform_rows(at, pattern, strip, low, high, real_table, pair_table, g_real, g_pair, re, im):
    span = pattern.shape[1] // RADIX
    width = low.shape[1]
    inner = strip.shape[1]
    step = 32
    root = math.sqrt(0.5)

    def octant(a, src):
        first = a * span
        if first < width:
            return low[src, first : first + span]
        if first < width + inner:
            return strip[src, first - width : first - width + span]
        return high[src, first - width - inner : first - width - inner + span]

    def fold(index, carry):
        src = pl.ds(pl.multiple_of(at + index * step, step), step)
        dst = pl.ds(pl.multiple_of(index * step, step), step)
        parts = [
            (pattern[src, a * span : (a + 1) * span] * octant(a, src)).astype(jnp.float32) for a in range(RADIX)
        ]
        s = [parts[a] + parts[a + 4] for a in range(4)]
        d = [parts[a] - parts[a + 4] for a in range(4)]
        even, odd = s[0] + s[2], s[1] + s[3]
        near, far = root * (d[1] - d[3]), root * (d[1] + d[3])

        def put(ref, lead, off, value):
            ref[lead, dst, off : off + span] = value.astype(jnp.bfloat16)

        put(g_real, 0, 0, even + odd)
        put(g_real, 1, 0, even - odd)
        put(g_pair, 0, 0, d[0] + near)
        put(g_pair, 0, span, -(d[2] + far))
        put(g_pair, 1, 0, s[0] - s[2])
        put(g_pair, 1, span, s[3] - s[1])
        put(g_pair, 2, 0, d[0] - near)
        put(g_pair, 2, span, d[2] - far)
        return carry

    lax.fori_loop(0, g_real.shape[1] // step, fold, 0)
    blocks = re.shape[0]
    re = re.reshape(blocks * RADIX, re.shape[2])
    im = im.reshape(blocks * RADIX, im.shape[2])
    for k, i in enumerate((0, RADIX // 2)):
        out = lax.dot_general(real_table[k], g_real[k], NT, preferred_element_type=jnp.float32)
        re[pl.ds(i, blocks, stride=RADIX), :] = out[:blocks]
        im[pl.ds(i, blocks, stride=RADIX), :] = out[blocks:]
    for k in range(RADIX // 2 - 1):
        out = lax.dot_general(pair_table[k], g_pair[k], NT, preferred_element_type=jnp.float32)
        for n, (ref, i) in enumerate(((re, k + 1), (im, k + 1), (re, RADIX - 1 - k), (im, RADIX - 1 - k))):
            ref[pl.ds(i, blocks, stride=RADIX), :] = out[n * blocks : (n + 1) * blocks]


def turn_tiles(first, asker, codes, phase, re, im, turned_re, turned_im):
    period = phase.shape[2]
    sets = codes.shape[1]

    def turn_set(g, carry):
        base = pl.multiple_of((first * sets + g) * RADIX * RADIX, RADIX * RADIX)
        for n in range(RADIX):
            tile = codes[asker, g, n]
            turn = phase[jnp.bitwise_and(tile, period - 1)]
            cos, sin = turn[0:1], turn[1:2]
            up = lax.shift_right_logical(tile, period.bit_length() - 1)
            x, y = re[up], im[up]
            rows = pl.ds(base + n, RADIX, stride=RADIX)
            turned_re[rows, :] = x * cos + y * sin
            turned_im[rows, :] = y * cos - x * sin
        return carry

    lax.fori_loop(0, sets, turn_set, 0, unroll=True)


def pick_cells(weights, turned_re, turned_im):
    rows, cells = turned_re.shape
    turned = jnp.concatenate([turned_re[...], turned_im[...]], axis=1).astype(jnp.bfloat16)
    cells_of = lax.dot_general(turned, weights, NN, preferred_element_type=jnp.float32)
    wide = cells_of.shape[1]
    cells_of = cells_of.reshape(rows // (RADIX * RADIX), RADIX, RADIX, wide)
    column = lax.broadcasted_iota(jnp.int32, (RADIX, wide), 1)
    row_of = (column % (wide // 2)) // WIDE
    picked = cells_of[:, 0]
    for i in range(1, RADIX):
        picked = jnp.where((row_of == i)[None], cells_of[:, i], picked)
    return picked.reshape(rows // RADIX, wide)


def predict_kernel(
    group, beams, tiles_dev,
    sky, pattern_in, kernels_in, observed_in, owner_in, place_in, counts_in, real_in, pair_in, phase_in, fine_in,
    coarse_in,
    residual, shared, hot,
    strip, low, high, pattern, kernels, observed, owner, place, counts, real_table, pair_table, phase, fine, coarse,
    table, code, codes, codes_s,
    g_real, g_pair, re, im, turned_re, turned_im, total, part, came, given, wide, narrow,
    local, halo_send, halo_recv, code_send, code_recv, part_send, part_recv, share_send, share_recv,
):
    beam = lax.axis_index("beam")
    me = group_index()
    vis, cells = kernels.shape[0], kernels.shape[1]
    width = low.shape[1]
    period = phase.shape[2]
    chunks = pattern.shape[0] // period
    chips, cores = lax.axis_size("bl"), lax.axis_size("pol")
    has_next, has_last = beam < beams - 1, beam > 0

    names = ("strip", "owner", "place", "phase", "fine", "coarse", "pattern", "real", "pair", "kernels", "observed", "counts")
    loads = {}
    for n, (name, src, dst) in enumerate(zip(names, (
        sky, owner_in, place_in, phase_in, fine_in, coarse_in.at[pl.ds(me * chunks, chunks)], pattern_in, real_in,
        pair_in, kernels_in, observed_in, counts_in,
    ), (
        strip, owner, place, phase, fine, coarse, pattern, real_table, pair_table, kernels, observed, counts,
    ))):
        loads[name] = pltpu.make_async_copy(src, dst, local.at[n])
        loads[name].start()

    orders = [(turn, core) for turn in range(1, chips + 1) for core in range(cores) if turn < chips or core > 0]
    barrier = pltpu.get_barrier_semaphore()

    def greet(device):
        pl.semaphore_signal(barrier, inc=1, device_id=device, device_id_type=MESH)

    for turn, core in orders:
        chip, side = chip_peer(turn, core)
        greet({"bl": chip, "pol": side})

    @pl.when(has_next)
    def _():
        greet({"beam": beam + 1})

    @pl.when(has_last)
    def _():
        greet({"beam": beam - 1})

    @pl.when(beam == 0)
    def _():
        low[...] = jnp.zeros_like(low)

    @pl.when(beam == beams - 1)
    def _():
        high[...] = jnp.zeros_like(high)

    total[...] = jnp.zeros_like(total)
    wide[...] = jnp.zeros_like(wide)
    loads["owner"].wait()
    loads["place"].wait()
    named = owner[...] * tiles_dev + place[...]
    named = jnp.concatenate([named] * (code.shape[1] // vis), axis=1)
    for g in range(vis // RADIX):
        code[g : g + 1, :] = named if g == 0 else pltpu.roll(named, code.shape[1] - g * RADIX, 1)
    loads["fine"].wait()
    loads["coarse"].wait()
    for k in range(chunks):
        cos_c, sin_c = coarse[k, 0:1], coarse[k, 1:2]
        cos = (fine[0] * cos_c - fine[1] * sin_c).astype(jnp.bfloat16)
        sin = (fine[1] * cos_c + fine[0] * sin_c).astype(jnp.bfloat16)
        table[k, :period, :cells] = cos
        table[k, :period, cells:] = -sin
        table[k, period:, :cells] = sin
        table[k, period:, cells:] = cos
    loads["strip"].wait()

    edges = jnp.where(beam < beams - 1, 1, 0) + jnp.where(beam > 0, 1, 0)
    with scope("barrier"):
        pl.semaphore_wait(barrier, group - 1 + edges)

    def halo(side, k):
        rows = pl.ds(pl.multiple_of(k * period, period), period)
        first = 0 if side else strip.shape[1] - width
        return pltpu.make_async_remote_copy(
            src_ref=strip.at[rows, pl.ds(first, width)], dst_ref=(high if side else low).at[rows, :],
            send_sem=halo_send.at[side, k], recv_sem=halo_recv.at[side, k],
            device_id={"beam": beam - 1 if side else beam + 1}, device_id_type=MESH,
        )

    def to_peer(turn, core, source, target, send, recv):
        chip, side = chip_peer(turn, core)
        slot = (turn - 1) * cores + core
        return pltpu.make_async_remote_copy(
            src_ref=source, dst_ref=target,
            send_sem=send.at[slot], recv_sem=recv.at[slot],
            device_id={"bl": chip, "pol": side}, device_id_type=MESH,
        )

    def index_of(turn, core):
        chip, side = chip_peer(turn, core)
        return chip * cores + side

    named_copies = [to_peer(turn, core, code, codes.at[me], code_send, code_recv) for turn, core in orders]
    for copy in named_copies:
        copy.start()

    @pl.when(has_next)
    def _():
        for k in range(chunks):
            halo(0, k).start()

    @pl.when(has_last)
    def _():
        for k in range(chunks):
            halo(1, k).start()

    codes[me] = code[...]
    with scope("codes"):
        for copy in named_copies:
            copy.wait()
    to_scalar = pltpu.make_async_copy(codes, codes_s, local.at[len(loads)])
    to_scalar.start()

    lanes = code.shape[1]
    each = lanes // vis
    lane = lax.broadcasted_iota(jnp.int32, (1, lanes), 1)
    keys = []
    for first in range(0, group, each):
        key = codes[first, 0:1, :]
        for n in range(1, each):
            key = jnp.where(lane < n * vis, key, codes[first + n, 0:1, :])
        keys.append(key)
    key = jnp.concatenate(keys, axis=1) - me * tiles_dev
    step = 256

    def heat(block, carry):
        at = pl.multiple_of(block * step, step)
        tile = lax.broadcasted_iota(jnp.int32, (step, key.shape[1]), 0)
        hot[pl.ds(at, step), :] = jnp.where(tile == key - at, 1.0, 0.0).astype(jnp.bfloat16)
        return carry

    with scope("heat"):
        lax.fori_loop(0, tiles_dev // step, heat, 0)
    to_scalar.wait()
    for name in ("phase", "pattern", "real", "pair"):
        loads[name].wait()

    def of_chunk(k, carry):
        with scope("halo"):

            @pl.when(has_last)
            def _():
                halo(0, k).wait_recv()

            @pl.when(has_next)
            def _():
                halo(1, k).wait_recv()

        with scope("rows"):
            transform_rows(k * period, pattern, strip, low, high, real_table, pair_table, g_real, g_pair, re, im)

        def of_chip(turn, inner):
            with scope("turn"):
                for core in range(cores):
                    turn_tiles(core, index_of(turn, core), codes_s, phase, re, im, turned_re, turned_im)
            picked = pick_cells(table[k], turned_re, turned_im)
            for core in range(cores):
                rows = pl.ds(pl.multiple_of(index_of(turn, core) * vis, vis), vis)
                total[rows, :] += picked[core * vis : (core + 1) * vis]

                @pl.when((k == chunks - 1) & ((turn < chips) | (core > 0)))
                def _():
                    part[rows, :] = total[rows, :].astype(part.dtype)
                    to_peer(turn, core, part.at[rows, :], came.at[me], part_send, part_recv).start()

            return inner

        lax.fori_loop(1, chips + 1, of_chip, 0)
        return carry

    lax.fori_loop(0, chunks, of_chunk, 0)

    loads["counts"].wait()
    loads["observed"].wait()
    own = lax.broadcasted_iota(jnp.int32, (vis, vis), 0) == lax.broadcasted_iota(jnp.int32, (vis, vis), 1)
    count = jnp.sum(jnp.where(own, counts[...].astype(jnp.float32), 0.0), axis=1, keepdims=True)
    mask = lax.broadcasted_iota(jnp.int32, (vis, cells), 1).astype(jnp.float32) < count
    mine = total[pl.ds(pl.multiple_of(me * vis, vis), vis), :]
    loads["kernels"].wait()
    with scope("parts"):
        for turn, core in orders:
            rows = pl.ds(pl.multiple_of(index_of(turn, core) * vis, vis), vis)
            to_peer(turn, core, part.at[rows, :], came.at[me], part_send, part_recv).wait()
    for turn, core in orders:
        mine = mine + came[index_of(turn, core)].astype(jnp.float32)
    for c in range(2):
        wide[pl.ds(c, vis, stride=RADIX), :] = mine[:, c * cells : (c + 1) * cells]

    def apply(dims):
        def of_tile(r, carry):
            at = pl.ds(pl.multiple_of(r * RADIX, RADIX), RADIX)
            narrow[at, :] = lax.dot_general(
                wide[at, :].astype(jnp.bfloat16), kernels[r], dims, preferred_element_type=jnp.float32
            )
            return carry

        lax.fori_loop(0, vis, of_tile, 0, unroll=True)

    with scope("nt"):
        apply(NT)
    for c in range(2):
        seen = observed[pl.ds(c, vis, stride=2), :]
        left = jnp.where(mask, seen - narrow[pl.ds(c, vis, stride=RADIX), :], 0.0)
        residual[pl.ds(c, vis, stride=2), :] = left
        wide[pl.ds(c, vis, stride=RADIX), :] = left
    with scope("nn"):
        apply(NN)
    for c in range(2):
        given[:, c * cells : (c + 1) * cells] = narrow[pl.ds(c, vis, stride=RADIX), :].astype(given.dtype)
    given_copies = [to_peer(turn, core, given, shared.at[me], share_send, share_recv) for turn, core in orders]
    for copy in given_copies:
        copy.start()
    shared[me] = given[...]
    with scope("given"):
        for copy in given_copies:
            copy.wait()

    @pl.when(has_next)
    def _():
        for k in range(chunks):
            halo(0, k).wait_send()

    @pl.when(has_last)
    def _():
        for k in range(chunks):
            halo(1, k).wait_send()


def dirty_kernel(hot, terms, left, dirty, residual, held, sems):
    blocks, rows, cells = held.shape
    rows = rows // 2
    kept = pltpu.make_async_copy(left, residual, sems.at[blocks])
    kept.start()
    copies = [kept]
    for block in range(blocks):
        out = lax.dot_general(
            hot[block * rows : (block + 1) * rows, :], terms[...], NN, preferred_element_type=jnp.float32
        )
        for c in range(2):
            held[block, pl.ds(c, rows, stride=2), :] = out[:, c * cells : (c + 1) * cells]
        copy = pltpu.make_async_copy(
            held.at[block], dirty.at[pl.ds(block * rows * 2, rows * 2), :], sems.at[block]
        )
        copy.start()
        copies.append(copy)
    for copy in copies:
        copy.wait()


def on_device(sky_model, beam_pattern, kernels, observed, tile_owner, tile_local, vis_count):
    group = lax.axis_size(("bl", "pol"))
    cores = lax.axis_size("pol")
    beams = lax.axis_size("beam")
    rows, grid = beam_pattern.shape[1:]
    strip = sky_model.shape[1]
    halo = (grid - strip) // 2
    vis, cells = kernels.shape[1], kernels.shape[3]
    tiles_dev = (grid // 2 // RADIX) * (grid // WIDE) // group
    lanes = 128
    f32, bf16, i32 = jnp.float32, jnp.bfloat16, jnp.int32
    real_table, pair_table = first_tables(grid)
    phase, fine, coarse = second_tables(grid)
    span, period = grid // RADIX, grid // WIDE
    chunks = rows // period
    dma = pltpu.SemaphoreType.DMA
    arrays = (
        sky_model, beam_pattern[0], kernels[0], observed.reshape(vis * 2, cells),
        tile_owner.reshape(1, vis), tile_local, vis_count,
        jnp.asarray(real_table), jnp.asarray(pair_table), jnp.asarray(phase), jnp.asarray(fine), jnp.asarray(coarse),
    )

    residual, shared, hot = pl.pallas_call(
        functools.partial(predict_kernel, group, beams, tiles_dev),
        out_shape=(
            pltpu.VMEM((vis * 2, cells), f32),
            pltpu.VMEM((group, vis, 2 * cells), bf16),
            pltpu.VMEM((tiles_dev, group * vis), bf16),
        ),
        in_specs=[HBM] * len(arrays),
        out_specs=(VMEM, VMEM, VMEM),
        scratch_shapes=[
            pltpu.VMEM((rows, strip), bf16),
            pltpu.VMEM((rows, halo), bf16),
            pltpu.VMEM((rows, halo), bf16),
            pltpu.VMEM((rows, grid), bf16),
            pltpu.VMEM((vis, cells, cells), bf16),
            pltpu.VMEM((vis * 2, cells), f32),
            pltpu.VMEM((1, vis), i32),
            pltpu.VMEM((1, vis), i32),
            pltpu.VMEM((1, vis), i32),
            pltpu.VMEM(real_table.shape, bf16),
            pltpu.VMEM(pair_table.shape, bf16),
            pltpu.VMEM(phase.shape, f32),
            pltpu.VMEM(fine.shape, f32),
            pltpu.VMEM((chunks, *coarse.shape[1:]), f32),
            pltpu.VMEM((chunks, 2 * period, 2 * cells), bf16),
            pltpu.VMEM((vis // RADIX, lanes), i32),
            pltpu.VMEM((group, vis // RADIX, lanes), i32),
            pltpu.SMEM((group, vis // RADIX, lanes), i32),
            pltpu.VMEM((2, period, span), bf16),
            pltpu.VMEM((RADIX // 2 - 1, period, 2 * span), bf16),
            pltpu.VMEM((grid // 2 // RADIX, RADIX, period), f32),
            pltpu.VMEM((grid // 2 // RADIX, RADIX, period), f32),
            pltpu.VMEM((cores * vis * RADIX, period), f32),
            pltpu.VMEM((cores * vis * RADIX, period), f32),
            pltpu.VMEM((group * vis, 2 * cells), f32),
            pltpu.VMEM((group * vis, 2 * cells), bf16),
            pltpu.VMEM((group, vis, 2 * cells), bf16),
            pltpu.VMEM((vis, 2 * cells), bf16),
            pltpu.VMEM((vis * RADIX, cells), f32),
            pltpu.VMEM((vis * RADIX, cells), f32),
            dma((len(arrays) + 1,)),
            dma((2, chunks)), dma((2, chunks)),
            dma((group,)), dma((group,)),
            dma((group,)), dma((group,)),
            dma((group,)), dma((group,)),
        ],
        compiler_params=pltpu.CompilerParams(
            collective_id=0, has_side_effects=True, vmem_limit_bytes=40 * 1024 * 1024
        ),
        name="predict",
    )(*[pltpu.with_memory_space_constraint(x, pltpu.HBM) for x in arrays])

    blocks = 8
    dirty, residual = pl.pallas_call(
        dirty_kernel,
        out_shape=(
            jax.ShapeDtypeStruct((tiles_dev * 2, cells), f32),
            jax.ShapeDtypeStruct((vis * 2, cells), f32),
        ),
        in_specs=[VMEM, VMEM, VMEM],
        out_specs=(HBM, HBM),
        scratch_shapes=[pltpu.VMEM((blocks, tiles_dev * 2 // blocks, cells), f32), dma((blocks + 1,))],
        compiler_params=pltpu.CompilerParams(vmem_limit_bytes=12 * 1024 * 1024),
        name="dirty",
    )(hot, shared.reshape(group * vis, 2 * cells), residual)
    return (
        residual.reshape(1, vis, 2, cells),
        dirty.reshape(1, tiles_dev, 2, cells),
    )


def solution(mesh):
    placed = (
        P(("tile", "bl", "pol"), "beam"),
        P(("tile", "beam"), ("bl", "pol"), None),
        P(("tile", "beam"), ("bl", "pol"), None, None),
        P(("tile", "beam"), ("bl", "pol"), None, None),
        P(("tile", "beam"), ("bl", "pol"), None),
        P(("tile", "beam"), ("bl", "pol")),
        P(("tile", "beam"), ("bl", "pol")),
    )
    return jax.shard_map(
        on_device,
        mesh=mesh,
        in_specs=placed,
        out_specs=(
            P(("tile", "beam"), ("bl", "pol"), None, None),
            P(("tile", "beam"), ("bl", "pol"), None, None),
        ),
        check_vma=False,
    )
```

time: 37.2 us -> 29.7 us (0.80)
  Pallas kernels: 36.4 us -> 28.9 us
    pallas_call x1, Pallas kernels: 32.5 us -> 26.5 us  [on_device(): pl.pallas_call(functools.partial(predict_kernel, group, beams, tiles_dev)...]
    pallas_call x1, Pallas kernels: 3.92 us -> 2.38 us  [on_device(): pl.pallas_call(dirty_kernel, out_shape=(jax.ShapeDtypeStruct((tiles_dev *...]
where the time goes in v1:
time: 29.7 us; the launch traced here: 29.5 us
  Pallas kernels  28.9 us (97%)
  between operations  0.64 us (2%)
    pallas_call x1, Pallas kernels, on_device(): pl.pallas_call(functools.partial(predict_kernel, group, beams, tiles_dev)...  26.5 us
    pallas_call x1, Pallas kernels, on_device(): pl.pallas_call(dirty_kernel, out_shape=(jax.ShapeDtypeStruct((tiles_dev *...  2.38 us

profile of v1, /device:TPU:0, one launch (start us, length us, event | category | flops | bytes accessed | tf_op | source)
XLA Modules:
  0.0 29.5 jit_solution(11495695034113903770)
XLA Ops:
  0.6 26.5 %predict.1 = (f32[128,128]{1,0:T(8,128)S(1)}, bf16[4,64,256]{2,1,0:T(8,128)(2,1)S(1)}, bf16[4096,256]{1,0:T(8,128)(2,1)S(1)}) custom-call(bf16[512,1024]{1,0:T(8,128)(2,1)} %sky.1, bf16[512,2048]{1,0:T(8,128)(2,1)} %bitcast.8, bf16[64,128,128]{2,1,0:T(8,128)(2,1)} %bitcast.9, f32[128,128]{1,0:T(8,128)} %bitcast.10, s32[1,64]{1,0:T(1,128)} %bitcast.11, ...), custom_call_target="tpu_custom_call" | custom-call | tf_op jit(solution)/shard_map/predict/pallas_call | solution.py:445
  27.1 2.4 %dirty.1 = (f32[8192,128]{1,0:T(8,128)}, f32[128,128]{1,0:T(8,128)}) custom-call(bf16[4096,256]{1,0:T(8,128)(2,1)S(1)} %get-tuple-element.7.hot, bf16[256,256]{1,0:T(8,128)(2,1)S(1)} %bitcast.7, f32[128,128]{1,0:T(8,128)S(1)} %get-tuple-element.9.left), custom_call_target="tpu_custom_call" | custom-call | tf_op jit(solution)/shard_map/dirty/pallas_call | solution.py:498

commit v2 on v1

v2 whole, which is shorter than its diff:
```python
import functools
import math

import jax
import jax.numpy as jnp
import numpy as np
from jax import lax
from jax.experimental import pallas as pl
from jax.experimental.pallas import tpu as pltpu
from jax.sharding import PartitionSpec as P

MESH = pl.DeviceIdType.MESH
RADIX = 8
WIDE = 16
PITCH = RADIX + 1
PIECES = 2
scope = jax.named_scope
VMEM = pl.BlockSpec(memory_space=pltpu.VMEM)
HBM = pl.BlockSpec(memory_space=pltpu.HBM)
NT = (((1,), (1,)), ((), ()))
NN = (((1,), (0,)), ((), ()))
TN = (((0,), (0,)), ((), ()))


def wave(rows, cols, period, factor):
    angle = (np.outer(rows, cols) % period) * (2.0 * math.pi / period)
    return np.cos(angle) * factor, np.sin(angle) * factor


def first_tables(grid):
    span = grid // RADIX
    blocks = grid // 2 // RADIX
    cols = np.arange(span)

    def of(i):
        return wave(RADIX * np.arange(blocks) + i, cols, grid, grid**-0.5)

    real = []
    for i in (0, RADIX // 2):
        cos, sin = of(i)
        real.append(np.concatenate([cos, -sin], 0))
    tables = [np.concatenate(real, 1)]
    for i in range(1, RADIX // 2):
        cos, sin = of(i)
        cos_m, sin_m = of(RADIX - i)
        tables.append(
            np.concatenate(
                [
                    np.concatenate([cos, sin], 1),
                    np.concatenate([-sin, cos], 1),
                    np.concatenate([cos_m, -sin_m], 1),
                    np.concatenate([-sin_m, -cos_m], 1),
                ],
                0,
            )
        )
    return np.concatenate(tables, 0).astype(jnp.bfloat16)


def second_tables(grid):
    period = grid // WIDE
    phase = np.stack(wave(np.arange(period), np.arange(period), period, 1.0), 1)
    cos, sin = wave(np.arange(period), np.arange(WIDE), grid, grid**-0.5)
    fine = [np.tile(cos, (1, RADIX)), np.tile(sin, (1, RADIX))]
    cos, sin = wave(np.arange(WIDE), np.arange(WIDE), WIDE, 1.0)
    coarse = np.stack([np.tile(cos, (1, RADIX)), np.tile(sin, (1, RADIX))], 1)
    waves = [phase.reshape(2 * period, -1), *fine, coarse.reshape(2 * WIDE, -1)]
    return np.concatenate(waves, 0).astype(np.float32)


def group_index():
    return lax.axis_index("bl") * lax.axis_size("pol") + lax.axis_index("pol")


class Slots:
    def __init__(self):
        self.chips, self.cores = lax.axis_size("bl"), lax.axis_size("pol")
        self.all = [(turn, core) for turn in range(1, self.chips + 1) for core in range(self.cores)]
        self.own = (self.chips, 0)
        self.peers = [pair for pair in self.all if pair != self.own]

    def number(self, pair):
        return (pair[0] - 1) * self.cores + pair[1]

    def device(self, pair):
        chip = lax.rem(lax.axis_index("bl") + pair[0], self.chips)
        return {"bl": chip, "pol": lax.rem(lax.axis_index("pol") + pair[1], self.cores)}

    def back(self, pair):
        turn = self.chips - pair[0] if pair[0] < self.chips else self.chips
        return turn, (self.cores - pair[1]) % self.cores


def transform_rows(at, pattern, strip, low, high, tables, g_real, g_pair, half):
    span = pattern.shape[1] // RADIX
    width = low.shape[1]
    inner = strip.shape[1]
    step = 32
    root = math.sqrt(0.5)

    def octant(a, src):
        first = a * span
        if first < width:
            return low[src, first : first + span]
        if first < width + inner:
            return strip[src, first - width : first - width + span]
        return high[src, first - width - inner : first - width - inner + span]

    def fold(index, carry):
        src = pl.ds(pl.multiple_of(at + index * step, step), step)
        dst = pl.ds(pl.multiple_of(index * step, step), step)
        parts = [
            (pattern[src, a * span : (a + 1) * span] * octant(a, src)).astype(jnp.float32) for a in range(RADIX)
        ]
        s = [parts[a] + parts[a + 4] for a in range(4)]
        d = [parts[a] - parts[a + 4] for a in range(4)]
        even, odd = s[0] + s[2], s[1] + s[3]
        near, far = root * (d[1] - d[3]), root * (d[1] + d[3])

        def put(ref, lead, off, value):
            ref[lead, dst, off : off + span] = value.astype(jnp.bfloat16)

        put(g_real, 0, 0, even + odd)
        put(g_real, 1, 0, even - odd)
        put(g_pair, 0, 0, d[0] + near)
        put(g_pair, 0, span, -(d[2] + far))
        put(g_pair, 1, 0, s[0] - s[2])
        put(g_pair, 1, span, s[3] - s[1])
        put(g_pair, 2, 0, d[0] - near)
        put(g_pair, 2, span, d[2] - far)
        return carry

    lax.fori_loop(0, g_real.shape[1] // step, fold, 0)
    blocks = half.shape[1] // PITCH
    re, im = half.at[0], half.at[1]
    for k, i in enumerate((0, RADIX // 2)):
        weights = tables[: 2 * blocks, k * span : (k + 1) * span]
        out = lax.dot_general(weights, g_real[k], NT, preferred_element_type=jnp.float32)
        re[pl.ds(i, blocks, stride=PITCH), :] = out[:blocks]
        im[pl.ds(i, blocks, stride=PITCH), :] = out[blocks:]
    for k in range(RADIX // 2 - 1):
        weights = tables[(2 + 4 * k) * blocks : (6 + 4 * k) * blocks]
        out = lax.dot_general(weights, g_pair[k], NT, preferred_element_type=jnp.float32)
        for n, (ref, i) in enumerate(((re, k + 1), (im, k + 1), (re, RADIX - 1 - k), (im, RADIX - 1 - k))):
            ref[pl.ds(i, blocks, stride=PITCH), :] = out[n * blocks : (n + 1) * blocks]


def turn_tiles(source, sets, codes, waves, half, turned_re, turned_im):
    lanes = codes.shape[2]

    def turn_set(g, carry):
        base = g * RADIX * PITCH
        for n in range(RADIX):
            at = codes[source, sets[0] + g, lanes // 2 + n]
            up = codes[source, sets[0] + g, n]
            cos, sin = waves[pl.ds(at, 1), :], waves[pl.ds(at + 1, 1), :]
            x, y = half[0, pl.ds(up, RADIX), :], half[1, pl.ds(up, RADIX), :]
            rows = pl.ds(base + n, RADIX, stride=PITCH)
            turned_re[rows, :] = x * cos + y * sin
            turned_im[rows, :] = y * cos - x * sin
        return carry

    lax.fori_loop(0, sets[1] - sets[0], turn_set, 0, unroll=True)


def pick_cells(count, weights, turned_re, turned_im):
    def rows_of(ref):
        return jnp.concatenate([ref[n * PITCH : n * PITCH + RADIX, :] for n in range(count * RADIX)], axis=0)

    turned = jnp.concatenate([rows_of(turned_re), rows_of(turned_im)], axis=1).astype(jnp.bfloat16)
    cells_of = lax.dot_general(turned, weights, NN, preferred_element_type=jnp.float32)
    wide = cells_of.shape[1]
    cells_of = cells_of.reshape(count, RADIX, RADIX, wide)
    column = lax.broadcasted_iota(jnp.int32, (RADIX, wide), 1)
    row_of = (column % (wide // 2)) // WIDE
    picked = cells_of[:, 0]
    for i in range(1, RADIX):
        picked = jnp.where((row_of == i)[None], cells_of[:, i], picked)
    return picked.reshape(count * RADIX, wide)


def predict_kernel(
    group, beams, tiles_dev,
    sky, pattern_in, kernels_in, observed_in, owner_in, place_in, counts_in, tables_in, waves_in,
    residual, shared, hot,
    strip, low, high, pattern, kernels, observed, owner, place, counts, counts_s, tables, waves,
    table, code, codes, split, codes_s,
    g_real, g_pair, half, turned_re, turned_im, total, part, came, given, wide, narrow, seen_wide, seen_rows, gram,
    local, halo_send, halo_recv, peer_send, code_recv, part_recv, share_recv,
):
    beam = lax.axis_index("beam")
    me = group_index()
    slots = Slots()
    vis, cells = kernels.shape[0], kernels.shape[1]
    width = low.shape[1]
    period = table.shape[1] // 2
    chunks = pattern.shape[0] // period
    has_next, has_last = beam < beams - 1, beam > 0

    strips = []
    for k in range(chunks):
        rows = pl.ds(k * period, period)
        strips.append(pltpu.make_async_copy(sky.at[rows], strip.at[rows], local.at[k]))
        strips[k].start()

    barrier = pltpu.get_barrier_semaphore()

    def greet(device):
        pl.semaphore_signal(barrier, inc=1, device_id=device, device_id_type=MESH)

    @pl.when(has_next)
    def _():
        greet({"beam": beam + 1})

    @pl.when(has_last)
    def _():
        greet({"beam": beam - 1})

    for pair in slots.peers:
        greet(slots.device(pair))

    loads = {}
    for n, (name, src, dst) in enumerate((
        ("owner", owner_in, owner), ("place", place_in, place), ("kernels", kernels_in, kernels),
        ("observed", observed_in, observed), ("counts", counts_in, counts), ("counts_s", counts_in, counts_s),
        ("waves", waves_in, waves), ("pattern", pattern_in, pattern), ("tables", tables_in, tables),
    )):
        loads[name] = pltpu.make_async_copy(src, dst, local.at[chunks + n])
        loads[name].start()

    strips[0].wait()
    edges = jnp.where(beam < beams - 1, 1, 0) + jnp.where(beam > 0, 1, 0)
    with scope("barrier"):
        pl.semaphore_wait(barrier, group - 1 + edges)

    def halo(side, k, count=1):
        rows = pl.ds(pl.multiple_of(k * period, period), count * period)
        first = 0 if side else strip.shape[1] - width
        return pltpu.make_async_remote_copy(
            src_ref=strip.at[rows, pl.ds(first, width)], dst_ref=(high if side else low).at[rows, :],
            send_sem=halo_send.at[side], recv_sem=halo_recv.at[side, k],
            device_id={"beam": beam - 1 if side else beam + 1}, device_id_type=MESH,
        )

    def to_peer(pair, piece, source, target, recv):
        n = slots.peers.index(pair)
        return pltpu.make_async_remote_copy(
            src_ref=source, dst_ref=target, send_sem=peer_send.at[piece, n], recv_sem=recv.at[piece, n],
            device_id=slots.device(pair), device_id_type=MESH,
        )

    early = lax.axis_index("pol") == 0
    for k in range(chunks):
        if k > 0:
            strips[k].wait()

        @pl.when(has_next & early)
        def _():
            halo(0, k).start()

        @pl.when(has_last & early)
        def _():
            halo(1, k).start()

    loads["owner"].wait()
    loads["place"].wait()
    named = owner[...] * tiles_dev + place[...]
    named = jnp.concatenate([named] * (code.shape[1] // vis), axis=1)
    for g in range(vis // RADIX):
        code[g : g + 1, :] = named if g == 0 else pltpu.roll(named, code.shape[1] - g * RADIX, 1)
    code_copies = [to_peer(pair, 0, code, codes.at[slots.number(pair)], code_recv) for pair in slots.peers]
    for copy in code_copies:
        copy.start()
    for k in range(chunks):

        @pl.when(has_next & jnp.logical_not(early))
        def _():
            halo(0, k).start()

        @pl.when(has_last & jnp.logical_not(early))
        def _():
            halo(1, k).start()

    codes[slots.number(slots.own)] = code[...]

    @pl.when(beam == 0)
    def _():
        low[...] = jnp.zeros_like(low)

    @pl.when(beam == beams - 1)
    def _():
        high[...] = jnp.zeros_like(high)

    total[...] = jnp.zeros_like(total)
    wide[...] = jnp.zeros_like(wide)
    seen_wide[...] = jnp.zeros_like(seen_wide)
    for name in ("waves", "kernels", "observed", "counts", "counts_s"):
        loads[name].wait()
    def spread(ref, first, count, c, value):
        rough = value.astype(jnp.bfloat16).astype(jnp.float32)
        ref[pl.ds(first * RADIX + c, count, stride=RADIX), :] = rough
        ref[pl.ds(first * RADIX + 2 + c, count, stride=RADIX), :] = value - rough

    def gathered(ref, first, count, c):
        rows = [ref[pl.ds(first * RADIX + c + d, count, stride=RADIX), :] for d in (0, 2)]
        return rows[0] + rows[1]

    def apply(matrices, dims, first, count):
        def of_tile(r, carry):
            at = pl.ds(pl.multiple_of(r * RADIX, RADIX), RADIX)
            narrow[at, :] = lax.dot_general(
                wide[at, :].astype(jnp.bfloat16), matrices[r], dims, preferred_element_type=jnp.float32
            )
            return carry

        lax.fori_loop(first, first + count, of_tile, 0, unroll=True)

    for k in range(chunks):
        row = 4 * period + 2 * (me * chunks + k)
        cos_c, sin_c = waves[pl.ds(row, 1), :], waves[pl.ds(row + 1, 1), :]
        cos_f, sin_f = waves[2 * period : 3 * period, :], waves[3 * period : 4 * period, :]
        cos = (cos_f * cos_c - sin_f * sin_c).astype(jnp.bfloat16)
        sin = (sin_f * cos_c + cos_f * sin_c).astype(jnp.bfloat16)
        table[k, :period, :cells] = cos
        table[k, :period, cells:] = -sin
        table[k, period:, :cells] = sin
        table[k, period:, cells:] = cos

    for c in range(2):
        spread(seen_wide, 0, vis, c, observed[pl.ds(c, vis, stride=2), :])
    row = lax.broadcasted_iota(jnp.int32, (cells, cells), 0)

    def gram_of(r, carry):
        at = pl.ds(pl.multiple_of(r * RADIX, RADIX), RADIX)
        kernel = kernels[r]
        live = jnp.where(row < counts_s[0, r], kernel.astype(jnp.float32), 0.0).astype(jnp.bfloat16)
        gram[r] = lax.dot_general(kernel, live, TN, preferred_element_type=jnp.float32).astype(jnp.bfloat16)
        seen_rows[at, :] = lax.dot_general(
            seen_wide[at, :].astype(jnp.bfloat16), live, NN, preferred_element_type=jnp.float32
        )
        return carry

    with scope("gram"):
        lax.fori_loop(0, vis, gram_of, 0, unroll=4)
    with scope("codes"):
        for copy in code_copies:
            copy.wait()
    lanes = code.shape[1]
    lane = lax.broadcasted_iota(jnp.int32, codes.shape, 2)
    up = lax.shift_right_logical(codes[...], period.bit_length() - 1)
    split[...] = jnp.where(lane < lanes // 2, up * PITCH, (codes[...] & (period - 1)) * 2)
    to_scalar = pltpu.make_async_copy(split, codes_s, local.at[0])
    to_scalar.start()

    fit = lanes // vis
    lane = lax.broadcasted_iota(jnp.int32, (1, lanes), 1)
    keys = []
    for first in range(0, group, fit):
        key = codes[first, 0:1, :]
        for n in range(1, fit):
            key = jnp.where(lane < n * vis, key, codes[first + n, 0:1, :])
        keys.append(key)
    key = jnp.concatenate(keys, axis=1) - me * tiles_dev
    step = 256

    def heat(block, carry):
        at = pl.multiple_of(block * step, step)
        tile = lax.broadcasted_iota(jnp.int32, (step, key.shape[1]), 0)
        hot[pl.ds(at, step), :] = jnp.where(tile == key - at, 1.0, 0.0).astype(jnp.bfloat16)
        return carry

    with scope("heat"):
        lax.fori_loop(0, tiles_dev // step, heat, 0)
    to_scalar.wait()
    for name in ("pattern", "tables"):
        loads[name].wait()

    each = vis // PIECES

    def span_of(pair, piece):
        first = slots.number(pair) * vis + piece * each
        return slice(first, first + each)

    def part_copy(pair, piece):
        target = came.at[slots.number(pair), pl.ds(piece * each, each)]
        return to_peer(pair, piece, part.at[span_of(pair, piece)], target, part_recv)

    def of_chunk(k, last):
        with scope("halo"):

            @pl.when(has_last)
            def _():
                halo(0, k).wait_recv()

            @pl.when(has_next)
            def _():
                halo(1, k).wait_recv()

        with scope("rows"):
            transform_rows(k * period, pattern, strip, low, high, tables, g_real, g_pair, half)
        far = [pair for pair in slots.all if pair[0] < slots.chips]
        near = [pair for pair in slots.all if pair[0] == slots.chips]
        for piece, pair in [(p, q) for some in (far, near) for p in range(PIECES) for q in some]:
            rows = span_of(pair, piece)
            at = slice(rows.start * PITCH, rows.stop * PITCH)
            re, im = turned_re.at[at], turned_im.at[at]
            sets = (piece * each // RADIX, (piece + 1) * each // RADIX)
            turn_tiles(slots.number(slots.back(pair)), sets, codes_s, waves, half, re, im)
            sums = total[rows, :] + pick_cells(each // RADIX, table[k], re, im)
            if last and pair != slots.own:
                part[rows, :] = sums.astype(part.dtype)
                part_copy(pair, piece).start()
            else:
                total[rows, :] = sums

    def chunk_loop(k, carry):
        of_chunk(k, False)
        return carry

    lax.fori_loop(0, chunks - 1, chunk_loop, 0)
    of_chunk(chunks - 1, True)

    given_copies = []
    for piece in range(PIECES):
        first = piece * each
        mine = total[span_of(slots.own, piece), :]
        with scope("parts"):
            for pair in slots.peers:
                part_copy(pair, piece).wait()
        for pair in slots.peers:
            mine = mine + came[slots.number(pair), first : first + each].astype(jnp.float32)
        for c in range(2):
            spread(wide, first, each, c, mine[:, c * cells : (c + 1) * cells])
        with scope("nn"):
            apply(gram, NN, first, each)
        for c in range(2):
            change = gathered(seen_rows, first, each, c) - gathered(narrow, first, each, c)
            given[first : first + each, c * cells : (c + 1) * cells] = change.astype(given.dtype)
        for pair in slots.peers:
            rows = pl.ds(first, each)
            copy = to_peer(pair, piece, given.at[rows], shared.at[slots.number(pair), rows], share_recv)
            copy.start()
            given_copies.append(copy)
        shared[slots.number(slots.own), first : first + each] = given[first : first + each]

    with scope("nt"):
        apply(kernels, NT, 0, vis)
    eye = lax.broadcasted_iota(jnp.int32, (vis, vis), 0) == lax.broadcasted_iota(jnp.int32, (vis, vis), 1)
    count = jnp.sum(jnp.where(eye, counts[...].astype(jnp.float32), 0.0), axis=1, keepdims=True)
    mask = lax.broadcasted_iota(jnp.int32, (vis, cells), 1).astype(jnp.float32) < count
    for c in range(2):
        seen = observed[pl.ds(c, vis, stride=2), :]
        residual[pl.ds(c, vis, stride=2), :] = jnp.where(mask, seen - gathered(narrow, 0, vis, c), 0.0)
    with scope("given"):
        for copy in given_copies:
            copy.wait()

    @pl.when(has_next)
    def _():
        halo(0, 0, chunks).wait_send()

    @pl.when(has_last)
    def _():
        halo(1, 0, chunks).wait_send()


def dirty_kernel(hot, terms, left, dirty, residual, held, sems):
    blocks, rows, cells = held.shape
    rows = rows // 2
    kept = pltpu.make_async_copy(left, residual, sems.at[blocks])
    kept.start()
    copies = [kept]
    for block in range(blocks):
        out = lax.dot_general(
            hot[block * rows : (block + 1) * rows, :], terms[...], NN, preferred_element_type=jnp.float32
        )
        for c in range(2):
            held[block, pl.ds(c, rows, stride=2), :] = out[:, c * cells : (c + 1) * cells]
        copy = pltpu.make_async_copy(
            held.at[block], dirty.at[pl.ds(block * rows * 2, rows * 2), :], sems.at[block]
        )
        copy.start()
        copies.append(copy)
    for copy in copies:
        copy.wait()


def on_device(sky_model, beam_pattern, kernels, observed, tile_owner, tile_local, vis_count):
    group = lax.axis_size(("bl", "pol"))
    beams = lax.axis_size("beam")
    rows, grid = beam_pattern.shape[1:]
    strip = sky_model.shape[1]
    halo = (grid - strip) // 2
    vis, cells = kernels.shape[1], kernels.shape[3]
    tiles_dev = (grid // 2 // RADIX) * (grid // WIDE) // group
    lanes = 128
    f32, bf16, i32 = jnp.float32, jnp.bfloat16, jnp.int32
    tables, waves = first_tables(grid), second_tables(grid)
    span, period = grid // RADIX, grid // WIDE
    chunks = rows // period
    dma = pltpu.SemaphoreType.DMA
    arrays = (
        sky_model, beam_pattern[0], kernels[0], observed.reshape(vis * 2, cells),
        tile_owner.reshape(1, vis), tile_local, vis_count,
        jnp.asarray(tables), jnp.asarray(waves),
    )

    residual, shared, hot = pl.pallas_call(
        functools.partial(predict_kernel, group, beams, tiles_dev),
        out_shape=(
            pltpu.VMEM((vis * 2, cells), f32),
            pltpu.VMEM((group, vis, 2 * cells), bf16),
            pltpu.VMEM((tiles_dev, group * vis), bf16),
        ),
        in_specs=[HBM] * len(arrays),
        out_specs=(VMEM, VMEM, VMEM),
        scratch_shapes=[
            pltpu.VMEM((rows, strip), bf16),
            pltpu.VMEM((rows, halo), bf16),
            pltpu.VMEM((rows, halo), bf16),
            pltpu.VMEM((rows, grid), bf16),
            pltpu.VMEM((vis, cells, cells), bf16),
            pltpu.VMEM((vis * 2, cells), f32),
            pltpu.VMEM((1, vis), i32),
            pltpu.VMEM((1, vis), i32),
            pltpu.VMEM((1, vis), i32),
            pltpu.SMEM((1, vis), i32),
            pltpu.VMEM(tables.shape, bf16),
            pltpu.VMEM(waves.shape, f32),
            pltpu.VMEM((chunks, 2 * period, 2 * cells), bf16),
            pltpu.VMEM((vis // RADIX, lanes), i32),
            pltpu.VMEM((group, vis // RADIX, lanes), i32),
            pltpu.VMEM((group, vis // RADIX, lanes), i32),
            pltpu.SMEM((group, vis // RADIX, lanes), i32),
            pltpu.VMEM((2, period, span), bf16),
            pltpu.VMEM((RADIX // 2 - 1, period, 2 * span), bf16),
            pltpu.VMEM((2, grid // 2 // RADIX * PITCH, period), f32),
            pltpu.VMEM((group * vis * PITCH, period), f32),
            pltpu.VMEM((group * vis * PITCH, period), f32),
            pltpu.VMEM((group * vis, 2 * cells), f32),
            pltpu.VMEM((group * vis, 2 * cells), bf16),
            pltpu.VMEM((group, vis, 2 * cells), bf16),
            pltpu.VMEM((vis, 2 * cells), bf16),
            pltpu.VMEM((vis * RADIX, cells), f32),
            pltpu.VMEM((vis * RADIX, cells), f32),
            pltpu.VMEM((vis * RADIX, cells), f32),
            pltpu.VMEM((vis * RADIX, cells), f32),
            pltpu.VMEM((vis, cells, cells), bf16),
            dma((len(arrays) + chunks,)),
            dma((2,)), dma((2, chunks)),
            dma((PIECES, group - 1)), dma((1, group - 1)), dma((PIECES, group - 1)), dma((PIECES, group - 1)),
        ],
        compiler_params=pltpu.CompilerParams(
            collective_id=0, has_side_effects=True, vmem_limit_bytes=40 * 1024 * 1024
        ),
        name="predict",
    )(*[pltpu.with_memory_space_constraint(x, pltpu.HBM) for x in arrays])

    blocks = 8
    dirty, residual = pl.pallas_call(
        dirty_kernel,
        out_shape=(
            jax.ShapeDtypeStruct((tiles_dev * 2, cells), f32),
            jax.ShapeDtypeStruct((vis * 2, cells), f32),
        ),
        in_specs=[VMEM, VMEM, VMEM],
        out_specs=(HBM, HBM),
        scratch_shapes=[pltpu.VMEM((blocks, tiles_dev * 2 // blocks, cells), f32), dma((blocks + 1,))],
        compiler_params=pltpu.CompilerParams(vmem_limit_bytes=12 * 1024 * 1024),
        name="dirty",
    )(hot, shared.reshape(group * vis, 2 * cells), residual)
    return (
        residual.reshape(1, vis, 2, cells),
        dirty.reshape(1, tiles_dev, 2, cells),
    )


def solution(mesh):
    placed = (
        P(("tile", "bl", "pol"), "beam"),
        P(("tile", "beam"), ("bl", "pol"), None),
        P(("tile", "beam"), ("bl", "pol"), None, None),
        P(("tile", "beam"), ("bl", "pol"), None, None),
        P(("tile", "beam"), ("bl", "pol"), None),
        P(("tile", "beam"), ("bl", "pol")),
        P(("tile", "beam"), ("bl", "pol")),
    )
    return jax.shard_map(
        on_device,
        mesh=mesh,
        in_specs=placed,
        out_specs=(
            P(("tile", "beam"), ("bl", "pol"), None, None),
            P(("tile", "beam"), ("bl", "pol"), None, None),
        ),
        check_vma=False,
    )
```

time: 29.7 us -> 28.2 us (0.949)
  Pallas kernels: 28.9 us -> 27.4 us
    pallas_call x1, Pallas kernels: 26.5 us -> 25.1 us  [on_device(): pl.pallas_call(functools.partial(predict_kernel, group, beams, tiles_dev)...]
where the time goes in v2:
time: 28.2 us; the launch traced here: 28.1 us
  Pallas kernels  27.4 us (97%)
  between operations  0.64 us (2%)
    pallas_call x1, Pallas kernels, on_device(): pl.pallas_call(functools.partial(predict_kernel, group, beams, tiles_dev)...  25.1 us
    pallas_call x1, Pallas kernels, on_device(): pl.pallas_call(dirty_kernel, out_shape=(jax.ShapeDtypeStruct((tiles_dev *...  2.38 us

profile of v2, /device:TPU:0, one launch (start us, length us, event | category | flops | bytes accessed | tf_op | source)
XLA Modules:
  0.0 28.1 jit_solution(15919320083647763183)
XLA Ops:
  0.6 25.1 %predict.1 = (f32[128,128]{1,0:T(8,128)S(1)}, bf16[4,64,256]{2,1,0:T(8,128)(2,1)S(1)}, bf16[4096,256]{1,0:T(8,128)(2,1)S(1)}) custom-call(bf16[512,1024]{1,0:T(8,128)(2,1)} %sky.1, bf16[512,2048]{1,0:T(8,128)(2,1)} %bitcast.8, bf16[64,128,128]{2,1,0:T(8,128)(2,1)} %bitcast.9, f32[128,128]{1,0:T(8,128)} %bitcast.10, s32[1,64]{1,0:T(1,128)} %bitcast.11, ...), custom_call_target="tpu_custom_call" | custom-call | tf_op jit(solution)/shard_map/predict/pallas_call | solution.py:508
  25.7 2.4 %dirty.1 = (f32[8192,128]{1,0:T(8,128)}, f32[128,128]{1,0:T(8,128)}) custom-call(bf16[4096,256]{1,0:T(8,128)(2,1)S(1)} %get-tuple-element.7.hot, bf16[256,256]{1,0:T(8,128)(2,1)S(1)} %bitcast.7, f32[128,128]{1,0:T(8,128)S(1)} %get-tuple-element.9.left), custom_call_target="tpu_custom_call" | custom-call | tf_op jit(solution)/shard_map/dirty/pallas_call | solution.py:560

commit v3 on v2

--- a/solution.py
+++ b/solution.py
@@ -39,21 +39,10 @@
     for i in (0, RADIX // 2):
         cos, sin = of(i)
         real.append(np.concatenate([cos, -sin], 0))
-    tables = [np.concatenate(real, 1)]
+    tables = list(real)
     for i in range(1, RADIX // 2):
-        cos, sin = of(i)
-        cos_m, sin_m = of(RADIX - i)
-        tables.append(
-            np.concatenate(
-                [
-                    np.concatenate([cos, sin], 1),
-                    np.concatenate([-sin, cos], 1),
-                    np.concatenate([cos_m, -sin_m], 1),
-                    np.concatenate([-sin_m, -cos_m], 1),
-                ],
-                0,
-            )
-        )
+        tables.extend(of(i))
+        tables.extend(of(RADIX - i))
     return np.concatenate(tables, 0).astype(jnp.bfloat16)
 
 
@@ -106,9 +95,10 @@
             return strip[src, first - width : first - width + span]
         return high[src, first - width - inner : first - width - inner + span]
 
+    count = g_real.shape[1]
+
     def fold(index, carry):
         src = pl.ds(pl.multiple_of(at + index * step, step), step)
-        dst = pl.ds(pl.multiple_of(index * step, step), step)
         parts = [
             (pattern[src, a * span : (a + 1) * span] * octant(a, src)).astype(jnp.float32) for a in range(RADIX)
         ]
@@ -117,32 +107,37 @@
         even, odd = s[0] + s[2], s[1] + s[3]
         near, far = root * (d[1] - d[3]), root * (d[1] + d[3])
 
-        def put(ref, lead, off, value):
-            ref[lead, dst, off : off + span] = value.astype(jnp.bfloat16)
+        def put(ref, lead, first, value):
+            ref[lead, pl.ds(pl.multiple_of(first + index * step, step), step), :] = value.astype(jnp.bfloat16)
 
         put(g_real, 0, 0, even + odd)
         put(g_real, 1, 0, even - odd)
+        put(g_pair, 1, 0, s[0] - s[2])
+        put(g_pair, 1, count, s[3] - s[1])
         put(g_pair, 0, 0, d[0] + near)
-        put(g_pair, 0, span, -(d[2] + far))
-        put(g_pair, 1, 0, s[0] - s[2])
-        put(g_pair, 1, span, s[3] - s[1])
+        put(g_pair, 0, count, -(d[2] + far))
         put(g_pair, 2, 0, d[0] - near)
-        put(g_pair, 2, span, d[2] - far)
+        put(g_pair, 2, count, d[2] - far)
         return carry
 
-    lax.fori_loop(0, g_real.shape[1] // step, fold, 0)
+    lax.fori_loop(0, count // step, fold, 0, unroll=True)
     blocks = half.shape[1] // PITCH
     re, im = half.at[0], half.at[1]
     for k, i in enumerate((0, RADIX // 2)):
-        weights = tables[: 2 * blocks, k * span : (k + 1) * span]
+        weights = tables[2 * k * blocks : 2 * (k + 1) * blocks]
         out = lax.dot_general(weights, g_real[k], NT, preferred_element_type=jnp.float32)
         re[pl.ds(i, blocks, stride=PITCH), :] = out[:blocks]
         im[pl.ds(i, blocks, stride=PITCH), :] = out[blocks:]
-    for k in range(RADIX // 2 - 1):
-        weights = tables[(2 + 4 * k) * blocks : (6 + 4 * k) * blocks]
+    for k in (1, 0, 2):
+        weights = tables[4 * (1 + k) * blocks : 4 * (2 + k) * blocks]
         out = lax.dot_general(weights, g_pair[k], NT, preferred_element_type=jnp.float32)
-        for n, (ref, i) in enumerate(((re, k + 1), (im, k + 1), (re, RADIX - 1 - k), (im, RADIX - 1 - k))):
-            ref[pl.ds(i, blocks, stride=PITCH), :] = out[n * blocks : (n + 1) * blocks]
+        parts = [[out[n * blocks : (n + 1) * blocks, c * count : (c + 1) * count] for c in range(2)] for n in range(4)]
+        (cos_re, cos_im), (sin_re, sin_im), (cos_re_m, cos_im_m), (sin_re_m, sin_im_m) = parts
+        at, mirror = pl.ds(k + 1, blocks, stride=PITCH), pl.ds(RADIX - 1 - k, blocks, stride=PITCH)
+        re[at, :] = cos_re + sin_im
+        im[at, :] = cos_im - sin_re
+        re[mirror, :] = cos_re_m - sin_im_m
+        im[mirror, :] = -sin_re_m - cos_im_m
 
 
 def turn_tiles(source, sets, codes, waves, half, turned_re, turned_im):
@@ -197,12 +192,6 @@
     chunks = pattern.shape[0] // period
     has_next, has_last = beam < beams - 1, beam > 0
 
-    strips = []
-    for k in range(chunks):
-        rows = pl.ds(k * period, period)
-        strips.append(pltpu.make_async_copy(sky.at[rows], strip.at[rows], local.at[k]))
-        strips[k].start()
-
     barrier = pltpu.get_barrier_semaphore()
 
     def greet(device):
@@ -218,6 +207,13 @@
 
     for pair in slots.peers:
         greet(slots.device(pair))
+
+    strips = []
+    for n, (first, rows) in enumerate(((0, period), (period, (chunks - 1) * period))):
+        if rows:
+            at = pl.ds(first, rows)
+            strips.append(pltpu.make_async_copy(sky.at[at], strip.at[at], local.at[n]))
+            strips[n].start()
 
     loads = {}
     for n, (name, src, dst) in enumerate((
@@ -225,7 +221,7 @@
         ("observed", observed_in, observed), ("counts", counts_in, counts), ("counts_s", counts_in, counts_s),
         ("waves", waves_in, waves), ("pattern", pattern_in, pattern), ("tables", tables_in, tables),
     )):
-        loads[name] = pltpu.make_async_copy(src, dst, local.at[chunks + n])
+        loads[name] = pltpu.make_async_copy(src, dst, local.at[2 + n])
         loads[name].start()
 
     strips[0].wait()
@@ -238,29 +234,35 @@
         first = 0 if side else strip.shape[1] - width
         return pltpu.make_async_remote_copy(
             src_ref=strip.at[rows, pl.ds(first, width)], dst_ref=(high if side else low).at[rows, :],
-            send_sem=halo_send.at[side], recv_sem=halo_recv.at[side, k],
+            send_sem=halo_send.at[side], recv_sem=halo_recv.at[k],
             device_id={"beam": beam - 1 if side else beam + 1}, device_id_type=MESH,
         )
 
-    def to_peer(pair, piece, source, target, recv):
-        n = slots.peers.index(pair)
+    def to_peer(pair, source, target, send, recv):
         return pltpu.make_async_remote_copy(
-            src_ref=source, dst_ref=target, send_sem=peer_send.at[piece, n], recv_sem=recv.at[piece, n],
+            src_ref=source, dst_ref=target, send_sem=send, recv_sem=recv,
             device_id=slots.device(pair), device_id_type=MESH,
         )
 
+    def wait_for(amount, sem):
+        pltpu.make_async_copy(amount, amount, sem).wait()
+
     early = lax.axis_index("pol") == 0
     for k in range(chunks):
-        if k > 0:
-            strips[k].wait()
+        if k == 1:
+            strips[1].wait()
 
         @pl.when(has_next & early)
         def _():
             halo(0, k).start()
 
-        @pl.when(has_last & early)
+        @pl.when(has_last)
         def _():
             halo(1, k).start()
+
+        @pl.when(has_next & jnp.logical_not(early))
+        def _():
+            halo(0, k).start()
 
     loads["owner"].wait()
     loads["place"].wait()
@@ -268,19 +270,8 @@
     named = jnp.concatenate([named] * (code.shape[1] // vis), axis=1)
     for g in range(vis // RADIX):
         code[g : g + 1, :] = named if g == 0 else pltpu.roll(named, code.shape[1] - g * RADIX, 1)
-    code_copies = [to_peer(pair, 0, code, codes.at[slots.number(pair)], code_recv) for pair in slots.peers]
-    for copy in code_copies:
-        copy.start()
-    for k in range(chunks):
-
-        @pl.when(has_next & jnp.logical_not(early))
-        def _():
-            halo(0, k).start()
-
-        @pl.when(has_last & jnp.logical_not(early))
-        def _():
-            halo(1, k).start()
-
+    for pair in slots.peers:
+        to_peer(pair, code, codes.at[slots.number(pair)], peer_send.at[0], code_recv).start()
     codes[slots.number(slots.own)] = code[...]
 
     @pl.when(beam == 0)
@@ -343,8 +334,8 @@
     with scope("gram"):
         lax.fori_loop(0, vis, gram_of, 0, unroll=4)
     with scope("codes"):
-        for copy in code_copies:
-            copy.wait()
+        wait_for(codes.at[pl.ds(0, group - 1)], code_recv)
+        wait_for(codes.at[pl.ds(0, group - 1)], peer_send.at[0])
     lanes = code.shape[1]
     lane = lax.broadcasted_iota(jnp.int32, codes.shape, 2)
     up = lax.shift_right_logical(codes[...], period.bit_length() - 1)
@@ -383,16 +374,22 @@
 
     def part_copy(pair, piece):
         target = came.at[slots.number(pair), pl.ds(piece * each, each)]
-        return to_peer(pair, piece, part.at[span_of(pair, piece)], target, part_recv)
+        return to_peer(pair, part.at[span_of(pair, piece)], target, peer_send.at[1], part_recv.at[piece])
 
     def of_chunk(k, last):
         with scope("halo"):
 
-            @pl.when(has_last)
+            @pl.when(has_last & has_next)
+            def _():
+                rows = pl.ds(pl.multiple_of(k * period, period), period)
+                both = strip.at[rows, pl.ds(0, 2 * width)]
+                wait_for(both, halo_recv.at[k])
+
+            @pl.when(has_last & jnp.logical_not(has_next))
             def _():
                 halo(0, k).wait_recv()
 
-            @pl.when(has_next)
+            @pl.when(has_next & jnp.logical_not(has_last))
             def _():
                 halo(1, k).wait_recv()
 
@@ -420,13 +417,11 @@
     lax.fori_loop(0, chunks - 1, chunk_loop, 0)
     of_chunk(chunks - 1, True)
 
-    given_copies = []
     for piece in range(PIECES):
         first = piece * each
         mine = total[span_of(slots.own, piece), :]
         with scope("parts"):
-            for pair in slots.peers:
-                part_copy(pair, piece).wait()
+            wait_for(came.at[pl.ds(0, group - 1), pl.ds(first, each)], part_recv.at[piece])
         for pair in slots.peers:
             mine = mine + came[slots.number(pair), first : first + each].astype(jnp.float32)
         for c in range(2):
@@ -438,9 +433,7 @@
             given[first : first + each, c * cells : (c + 1) * cells] = change.astype(given.dtype)
         for pair in slots.peers:
             rows = pl.ds(first, each)
-            copy = to_peer(pair, piece, given.at[rows], shared.at[slots.number(pair), rows], share_recv)
-            copy.start()
-            given_copies.append(copy)
+            to_peer(pair, given.at[rows], shared.at[slots.number(pair), rows], peer_send.at[2], share_recv).start()
         shared[slots.number(slots.own), first : first + each] = given[first : first + each]
 
     with scope("nt"):
@@ -452,8 +445,9 @@
         seen = observed[pl.ds(c, vis, stride=2), :]
         residual[pl.ds(c, vis, stride=2), :] = jnp.where(mask, seen - gathered(narrow, 0, vis, c), 0.0)
     with scope("given"):
-        for copy in given_copies:
-            copy.wait()
+        wait_for(shared.at[pl.ds(0, group - 1)], share_recv)
+    wait_for(shared.at[pl.ds(0, group - 1)], peer_send.at[2])
+    wait_for(came.at[pl.ds(0, group - 1)], peer_send.at[1])
 
     @pl.when(has_next)
     def _():
@@ -464,25 +458,21 @@
         halo(1, 0, chunks).wait_send()
 
 
-def dirty_kernel(hot, terms, left, dirty, residual, held, sems):
-    blocks, rows, cells = held.shape
-    rows = rows // 2
-    kept = pltpu.make_async_copy(left, residual, sems.at[blocks])
+def dirty_kernel(blocks, hot, terms, left, dirty, residual, held, sems):
+    rows = held.shape[0] // blocks
+    cells = held.shape[1]
+    kept = pltpu.make_async_copy(left, residual, sems.at[1])
     kept.start()
-    copies = [kept]
     for block in range(blocks):
+        at = pl.ds(block * rows, rows)
         out = lax.dot_general(
-            hot[block * rows : (block + 1) * rows, :], terms[...], NN, preferred_element_type=jnp.float32
+            hot[block * rows // 2 : (block + 1) * rows // 2, :], terms[...], NN, preferred_element_type=jnp.float32
         )
         for c in range(2):
-            held[block, pl.ds(c, rows, stride=2), :] = out[:, c * cells : (c + 1) * cells]
-        copy = pltpu.make_async_copy(
-            held.at[block], dirty.at[pl.ds(block * rows * 2, rows * 2), :], sems.at[block]
-        )
-        copy.start()
-        copies.append(copy)
-    for copy in copies:
-        copy.wait()
+            held[pl.ds(block * rows + c, rows // 2, stride=2), :] = out[:, c * cells : (c + 1) * cells]
+        pltpu.make_async_copy(held.at[at], dirty.at[at], sems.at[0]).start()
+    pltpu.make_async_copy(held, dirty, sems.at[0]).wait()
+    kept.wait()
 
 
 def on_device(sky_model, beam_pattern, kernels, observed, tile_owner, tile_local, vis_count):
@@ -533,7 +523,7 @@
             pltpu.VMEM((group, vis // RADIX, lanes), i32),
             pltpu.SMEM((group, vis // RADIX, lanes), i32),
             pltpu.VMEM((2, period, span), bf16),
-            pltpu.VMEM((RADIX // 2 - 1, period, 2 * span), bf16),
+            pltpu.VMEM((RADIX // 2 - 1, 2 * period, span), bf16),
             pltpu.VMEM((2, grid // 2 // RADIX * PITCH, period), f32),
             pltpu.VMEM((group * vis * PITCH, period), f32),
             pltpu.VMEM((group * vis * PITCH, period), f32),
@@ -546,9 +536,8 @@
             pltpu.VMEM((vis * RADIX, cells), f32),
             pltpu.VMEM((vis * RADIX, cells), f32),
             pltpu.VMEM((vis, cells, cells), bf16),
-            dma((len(arrays) + chunks,)),
-            dma((2,)), dma((2, chunks)),
-            dma((PIECES, group - 1)), dma((1, group - 1)), dma((PIECES, group - 1)), dma((PIECES, group - 1)),
+            dma((len(arrays) + 2,)),
+            dma((2,)), dma((chunks,)), dma((3,)), dma, dma((PIECES,)), dma,
         ],
         compiler_params=pltpu.CompilerParams(
             collective_id=0, has_side_effects=True, vmem_limit_bytes=40 * 1024 * 1024
@@ -556,16 +545,15 @@
         name="predict",
     )(*[pltpu.with_memory_space_constraint(x, pltpu.HBM) for x in arrays])
 
-    blocks = 8
     dirty, residual = pl.pallas_call(
-        dirty_kernel,
+        functools.partial(dirty_kernel, 16),
         out_shape=(
             jax.ShapeDtypeStruct((tiles_dev * 2, cells), f32),
             jax.ShapeDtypeStruct((vis * 2, cells), f32),
         ),
         in_specs=[VMEM, VMEM, VMEM],
         out_specs=(HBM, HBM),
-        scratch_shapes=[pltpu.VMEM((blocks, tiles_dev * 2 // blocks, cells), f32), dma((blocks + 1,))],
+        scratch_shapes=[pltpu.VMEM((tiles_dev * 2, cells), f32), dma((2,))],
         compiler_params=pltpu.CompilerParams(vmem_limit_bytes=12 * 1024 * 1024),
         name="dirty",
     )(hot, shared.reshape(group * vis, 2 * cells), residual)

time: 28.2 us -> 27.3 us (0.968)
  Pallas kernels: 27.4 us -> 26.5 us
    pallas_call x1, Pallas kernels: 25.1 us -> 24.3 us  [on_device(): pl.pallas_call(functools.partial(predict_kernel, group, beams, tiles_dev)...]
where the time goes in v3:
time: 27.3 us; the launch traced here: 27.2 us
  Pallas kernels  26.5 us (97%)
  between operations  0.64 us (2%)
    pallas_call x1, Pallas kernels, on_device(): pl.pallas_call(functools.partial(predict_kernel, group, beams, tiles_dev)...  24.3 us
    pallas_call x1, Pallas kernels, on_device(): pl.pallas_call(functools.partial(dirty_kernel, 16), out_shape=(jax.ShapeD...  2.24 us

profile of v3, /device:TPU:0, one launch (start us, length us, event | category | flops | bytes accessed | tf_op | source)
XLA Modules:
  0.0 27.2 jit_solution(1448988276039398899)
XLA Ops:
  0.6 24.3 %predict.1 = (f32[128,128]{1,0:T(8,128)S(1)}, bf16[4,64,256]{2,1,0:T(8,128)(2,1)S(1)}, bf16[4096,256]{1,0:T(8,128)(2,1)S(1)}) custom-call(bf16[512,1024]{1,0:T(8,128)(2,1)} %sky.1, bf16[512,2048]{1,0:T(8,128)(2,1)} %bitcast.8, bf16[64,128,128]{2,1,0:T(8,128)(2,1)} %bitcast.9, f32[128,128]{1,0:T(8,128)} %bitcast.10, s32[1,64]{1,0:T(1,128)} %bitcast.11, ...), custom_call_target="tpu_custom_call" | custom-call | tf_op jit(solution)/shard_map/predict/pallas_call | solution.py:498
  24.9 2.2 %dirty.1 = (f32[8192,128]{1,0:T(8,128)}, f32[128,128]{1,0:T(8,128)}) custom-call(bf16[4096,256]{1,0:T(8,128)(2,1)S(1)} %get-tuple-element.7.hot, bf16[256,256]{1,0:T(8,128)(2,1)S(1)} %bitcast.7, f32[128,128]{1,0:T(8,128)S(1)} %get-tuple-element.9.left), custom_call_target="tpu_custom_call" | custom-call | tf_op jit(solution)/shard_map/dirty/pallas_call | solution.py:548

commit v4 on v3

--- a/solution.py
+++ b/solution.py
@@ -13,7 +13,7 @@
 RADIX = 8
 WIDE = 16
 PITCH = RADIX + 1
-PIECES = 2
+PIECES = 4
 scope = jax.named_scope
 VMEM = pl.BlockSpec(memory_space=pltpu.VMEM)
 HBM = pl.BlockSpec(memory_space=pltpu.HBM)
@@ -67,6 +67,7 @@
         self.all = [(turn, core) for turn in range(1, self.chips + 1) for core in range(self.cores)]
         self.own = (self.chips, 0)
         self.peers = [pair for pair in self.all if pair != self.own]
+        self.halves = self.chips == 2 and self.cores == 2
 
     def number(self, pair):
         return (pair[0] - 1) * self.cores + pair[1]
@@ -74,6 +75,11 @@
     def device(self, pair):
         chip = lax.rem(lax.axis_index("bl") + pair[0], self.chips)
         return {"bl": chip, "pol": lax.rem(lax.axis_index("pol") + pair[1], self.cores)}
+
+    def wants(self, pair, piece):
+        if not self.halves or pair[0] == self.chips:
+            return True
+        return (piece < PIECES // 2) == (pair[1] == 0)
 
     def back(self, pair):
         turn = self.chips - pair[0] if pair[0] < self.chips else self.chips
@@ -140,6 +146,29 @@
         im[mirror, :] = -sin_re_m - cos_im_m
 
 
+def sorted_tiles(owner, place, tiles_dev, firsts):
+    vis = owner.shape[1]
+    index = lax.broadcasted_iota(jnp.int32, (1, vis), 1)
+    none = jnp.zeros((1, vis), jnp.int32)
+
+    def count(r, heads):
+        return heads + jnp.where(owner[0, r] == firsts[0], 1, 0)
+
+    def put(r, carry):
+        head, tail, middle, named, tile, moved = carry
+        name = owner[0, r]
+        is_head, is_tail = jnp.where(name == firsts[0], 1, 0), jnp.where(name == firsts[1], 1, 0)
+        at = is_head * head + is_tail * tail + (1 - is_head - is_tail) * middle
+        here = index == at
+        named = jnp.where(here, name * tiles_dev + place[0, r], named)
+        tile = jnp.where(here, r, tile)
+        moved = jnp.where(index == r, at, moved)
+        return head + is_head, tail - is_tail, middle + 1 - is_head - is_tail, named, tile, moved
+
+    heads = lax.fori_loop(0, vis, count, jnp.int32(0), unroll=8)
+    return lax.fori_loop(0, vis, put, (jnp.int32(0), jnp.int32(vis - 1), heads, none, none, none), unroll=8)[3:]
+
+
 def turn_tiles(source, sets, codes, waves, half, turned_re, turned_im):
     lanes = codes.shape[2]
 
@@ -158,11 +187,16 @@
     lax.fori_loop(0, sets[1] - sets[0], turn_set, 0, unroll=True)
 
 
-def pick_cells(count, weights, turned_re, turned_im):
-    def rows_of(ref):
-        return jnp.concatenate([ref[n * PITCH : n * PITCH + RADIX, :] for n in range(count * RADIX)], axis=0)
-
-    turned = jnp.concatenate([rows_of(turned_re), rows_of(turned_im)], axis=1).astype(jnp.bfloat16)
+def pick_cells(weights, turned):
+    count = sum(re.shape[0] for re, _ in turned) // (RADIX * PITCH)
+
+    def rows_of(n):
+        refs = [pair[n] for pair in turned]
+        return jnp.concatenate(
+            [ref[at : at + RADIX, :] for ref in refs for at in range(0, ref.shape[0], PITCH)], axis=0
+        )
+
+    turned = jnp.concatenate([rows_of(0), rows_of(1)], axis=1).astype(jnp.bfloat16)
     cells_of = lax.dot_general(turned, weights, NN, preferred_element_type=jnp.float32)
     wide = cells_of.shape[1]
     cells_of = cells_of.reshape(count, RADIX, RADIX, wide)
@@ -179,7 +213,7 @@
     sky, pattern_in, kernels_in, observed_in, owner_in, place_in, counts_in, tables_in, waves_in,
     residual, shared, hot,
     strip, low, high, pattern, kernels, observed, owner, place, counts, counts_s, tables, waves,
-    table, code, codes, split, codes_s,
+    table, code, codes, split, codes_s, order, order_s,
     g_real, g_pair, half, turned_re, turned_im, total, part, came, given, wide, narrow, seen_wide, seen_rows, gram,
     local, halo_send, halo_recv, peer_send, code_recv, part_recv, share_recv,
 ):
@@ -266,7 +300,14 @@
 
     loads["owner"].wait()
     loads["place"].wait()
-    named = owner[...] * tiles_dev + place[...]
+    firsts = [slots.device(pair) for pair in slots.all if pair[0] < slots.chips]
+    firsts = [first["bl"] * slots.cores + first["pol"] for first in firsts] if slots.halves else [-1, -1]
+    named, tile, moved = sorted_tiles(owner, place, tiles_dev, firsts)
+    rows = (tile, tile * RADIX, moved * RADIX)
+    for n, row in enumerate(rows):
+        order[n : n + 1, :] = row
+    order_copy = pltpu.make_async_copy(order, order_s, local.at[1])
+    order_copy.start()
     named = jnp.concatenate([named] * (code.shape[1] // vis), axis=1)
     for g in range(vis // RADIX):
         code[g : g + 1, :] = named if g == 0 else pltpu.roll(named, code.shape[1] - g * RADIX, 1)
@@ -282,6 +323,13 @@
     def _():
         high[...] = jnp.zeros_like(high)
 
+    order_copy.wait()
+    for pair in slots.peers:
+        for piece in range(PIECES):
+            if not slots.wants(pair, piece):
+                each = vis // PIECES
+                rows = pl.ds(piece * each, each)
+                shared[slots.number(pair), rows] = jnp.zeros((each, shared.shape[2]), shared.dtype)
     total[...] = jnp.zeros_like(total)
     wide[...] = jnp.zeros_like(wide)
     seen_wide[...] = jnp.zeros_like(seen_wide)
@@ -296,15 +344,21 @@
         rows = [ref[pl.ds(first * RADIX + c + d, count, stride=RADIX), :] for d in (0, 2)]
         return rows[0] + rows[1]
 
-    def apply(matrices, dims, first, count):
-        def of_tile(r, carry):
-            at = pl.ds(pl.multiple_of(r * RADIX, RADIX), RADIX)
-            narrow[at, :] = lax.dot_general(
-                wide[at, :].astype(jnp.bfloat16), matrices[r], dims, preferred_element_type=jnp.float32
-            )
-            return carry
-
-        lax.fori_loop(first, first + count, of_tile, 0, unroll=True)
+    def rows_at(r):
+        return pl.ds(pl.multiple_of(r * RADIX, RADIX), RADIX)
+
+    def change_of(p, carry):
+        seen = seen_rows[pl.ds(order_s[1, p], RADIX), :]
+        narrow[rows_at(p), :] = seen - lax.dot_general(
+            wide[rows_at(p), :].astype(jnp.bfloat16), gram[order_s[0, p]], NN, preferred_element_type=jnp.float32
+        )
+        return carry
+
+    def predict_of(r, carry):
+        narrow[rows_at(r), :] = lax.dot_general(
+            wide[pl.ds(order_s[2, r], RADIX), :].astype(jnp.bfloat16), kernels[r], NT, preferred_element_type=jnp.float32
+        )
+        return carry
 
     for k in range(chunks):
         row = 4 * period + 2 * (me * chunks + k)
@@ -395,20 +449,27 @@
 
         with scope("rows"):
             transform_rows(k * period, pattern, strip, low, high, tables, g_real, g_pair, half)
-        far = [pair for pair in slots.all if pair[0] < slots.chips]
-        near = [pair for pair in slots.all if pair[0] == slots.chips]
-        for piece, pair in [(p, q) for some in (far, near) for p in range(PIECES) for q in some]:
-            rows = span_of(pair, piece)
-            at = slice(rows.start * PITCH, rows.stop * PITCH)
-            re, im = turned_re.at[at], turned_im.at[at]
-            sets = (piece * each // RADIX, (piece + 1) * each // RADIX)
-            turn_tiles(slots.number(slots.back(pair)), sets, codes_s, waves, half, re, im)
-            sums = total[rows, :] + pick_cells(each // RADIX, table[k], re, im)
-            if last and pair != slots.own:
-                part[rows, :] = sums.astype(part.dtype)
-                part_copy(pair, piece).start()
-            else:
-                total[rows, :] = sums
+        for turn in range(1, slots.chips + 1):
+            pairs = [pair for pair in slots.all if pair[0] == turn]
+            for piece in range(PIECES):
+                sets = (piece * each // RADIX, (piece + 1) * each // RADIX)
+                turned = []
+                for pair in pairs:
+                    rows = span_of(pair, piece)
+                    at = slice(rows.start * PITCH, rows.stop * PITCH)
+                    turned.append((turned_re.at[at], turned_im.at[at]))
+                    turn_tiles(slots.number(slots.back(pair)), sets, codes_s, waves, half, *turned[-1])
+                picked = pick_cells(table[k], turned)
+                for n, pair in enumerate(pairs):
+                    rows = span_of(pair, piece)
+                    sums = total[rows, :] + picked[n * each : (n + 1) * each]
+                    if last and pair != slots.own:
+                        part[rows, :] = sums.astype(part.dtype)
+                    else:
+                        total[rows, :] = sums
+                for pair in pairs:
+                    if last and pair != slots.own:
+                        part_copy(pair, piece).start()
 
     def chunk_loop(k, carry):
         of_chunk(k, False)
@@ -427,17 +488,18 @@
         for c in range(2):
             spread(wide, first, each, c, mine[:, c * cells : (c + 1) * cells])
         with scope("nn"):
-            apply(gram, NN, first, each)
+            lax.fori_loop(first, first + each, change_of, 0, unroll=True)
         for c in range(2):
-            change = gathered(seen_rows, first, each, c) - gathered(narrow, first, each, c)
+            change = gathered(narrow, first, each, c)
             given[first : first + each, c * cells : (c + 1) * cells] = change.astype(given.dtype)
         for pair in slots.peers:
             rows = pl.ds(first, each)
-            to_peer(pair, given.at[rows], shared.at[slots.number(pair), rows], peer_send.at[2], share_recv).start()
+            if slots.wants(pair, piece):
+                to_peer(pair, given.at[rows], shared.at[slots.number(pair), rows], peer_send.at[2], share_recv).start()
         shared[slots.number(slots.own), first : first + each] = given[first : first + each]
 
     with scope("nt"):
-        apply(kernels, NT, 0, vis)
+        lax.fori_loop(0, vis, predict_of, 0, unroll=True)
     eye = lax.broadcasted_iota(jnp.int32, (vis, vis), 0) == lax.broadcasted_iota(jnp.int32, (vis, vis), 1)
     count = jnp.sum(jnp.where(eye, counts[...].astype(jnp.float32), 0.0), axis=1, keepdims=True)
     mask = lax.broadcasted_iota(jnp.int32, (vis, cells), 1).astype(jnp.float32) < count
@@ -445,8 +507,9 @@
         seen = observed[pl.ds(c, vis, stride=2), :]
         residual[pl.ds(c, vis, stride=2), :] = jnp.where(mask, seen - gathered(narrow, 0, vis, c), 0.0)
     with scope("given"):
-        wait_for(shared.at[pl.ds(0, group - 1)], share_recv)
-    wait_for(shared.at[pl.ds(0, group - 1)], peer_send.at[2])
+        sent = sum(slots.wants(pair, piece) for pair in slots.peers for piece in range(PIECES)) // PIECES
+        wait_for(shared.at[pl.ds(0, sent)], share_recv)
+    wait_for(shared.at[pl.ds(0, sent)], peer_send.at[2])
     wait_for(came.at[pl.ds(0, group - 1)], peer_send.at[1])
 
     @pl.when(has_next)
@@ -458,19 +521,20 @@
         halo(1, 0, chunks).wait_send()
 
 
-def dirty_kernel(blocks, hot, terms, left, dirty, residual, held, sems):
-    rows = held.shape[0] // blocks
+def dirty_kernel(hot, terms, left, dirty, residual, held, sems):
+    tiles, terms_of = hot.shape
     cells = held.shape[1]
     kept = pltpu.make_async_copy(left, residual, sems.at[1])
     kept.start()
-    for block in range(blocks):
-        at = pl.ds(block * rows, rows)
-        out = lax.dot_general(
-            hot[block * rows // 2 : (block + 1) * rows // 2, :], terms[...], NN, preferred_element_type=jnp.float32
-        )
+    first, count = 0, tiles // 64
+    while first < tiles:
+        out = lax.dot_general(hot[first : first + count, :], terms[...], NN, preferred_element_type=jnp.float32)
         for c in range(2):
-            held[pl.ds(block * rows + c, rows // 2, stride=2), :] = out[:, c * cells : (c + 1) * cells]
+            held[pl.ds(2 * first + c, count, stride=2), :] = out[:, c * cells : (c + 1) * cells]
+        at = pl.ds(2 * first, 2 * count)
         pltpu.make_async_copy(held.at[at], dirty.at[at], sems.at[0]).start()
+        first += count
+        count = min(tiles - first, first, tiles // 16)
     pltpu.make_async_copy(held, dirty, sems.at[0]).wait()
     kept.wait()
 
@@ -511,8 +575,8 @@
             pltpu.VMEM((rows, grid), bf16),
             pltpu.VMEM((vis, cells, cells), bf16),
             pltpu.VMEM((vis * 2, cells), f32),
-            pltpu.VMEM((1, vis), i32),
-            pltpu.VMEM((1, vis), i32),
+            pltpu.SMEM((1, vis), i32),
+            pltpu.SMEM((1, vis), i32),
             pltpu.VMEM((1, vis), i32),
             pltpu.SMEM((1, vis), i32),
             pltpu.VMEM(tables.shape, bf16),
@@ -522,6 +586,8 @@
             pltpu.VMEM((group, vis // RADIX, lanes), i32),
             pltpu.VMEM((group, vis // RADIX, lanes), i32),
             pltpu.SMEM((group, vis // RADIX, lanes), i32),
+            pltpu.VMEM((3, vis), i32),
+            pltpu.SMEM((3, vis), i32),
             pltpu.VMEM((2, period, span), bf16),
             pltpu.VMEM((RADIX // 2 - 1, 2 * period, span), bf16),
             pltpu.VMEM((2, grid // 2 // RADIX * PITCH, period), f32),
@@ -546,7 +612,7 @@
     )(*[pltpu.with_memory_space_constraint(x, pltpu.HBM) for x in arrays])
 
     dirty, residual = pl.pallas_call(
-        functools.partial(dirty_kernel, 16),
+        dirty_kernel,
         out_shape=(
             jax.ShapeDtypeStruct((tiles_dev * 2, cells), f32),
             jax.ShapeDtypeStruct((vis * 2, cells), f32),

time: 27.3 us -> 26.8 us (0.982)
  Pallas kernels: 26.5 us -> 26 us
    pallas_call x1, Pallas kernels: 24.3 us -> 23.8 us  [on_device(): pl.pallas_call(functools.partial(predict_kernel, group, beams, tiles_dev)...]
where the time goes in v4:
time: 26.8 us; the launch traced here: 26.6 us
  Pallas kernels  26 us (97%)
  between operations  0.64 us (2%)
    pallas_call x1, Pallas kernels, on_device(): pl.pallas_call(functools.partial(predict_kernel, group, beams, tiles_dev)...  23.8 us
    pallas_call x1, Pallas kernels, on_device(): pl.pallas_call(dirty_kernel, out_shape=(jax.ShapeDtypeStruct((tiles_dev *...  2.22 us

profile of v4, /device:TPU:0, one launch (start us, length us, event | category | flops | bytes accessed | tf_op | source)
XLA Modules:
  0.0 26.6 jit_solution(15779410029702234972)
XLA Ops:
  0.6 23.8 %predict.1 = (f32[128,128]{1,0:T(8,128)S(1)}, bf16[4,64,256]{2,1,0:T(8,128)(2,1)S(1)}, bf16[4096,256]{1,0:T(8,128)(2,1)S(1)}) custom-call(bf16[512,1024]{1,0:T(8,128)(2,1)} %sky.1, bf16[512,2048]{1,0:T(8,128)(2,1)} %bitcast.8, bf16[64,128,128]{2,1,0:T(8,128)(2,1)} %bitcast.9, f32[128,128]{1,0:T(8,128)} %bitcast.10, s32[1,64]{1,0:T(1,128)} %bitcast.11, ...), custom_call_target="tpu_custom_call" | custom-call | tf_op jit(solution)/shard_map/predict/pallas_call | solution.py:562
  24.4 2.2 %dirty.1 = (f32[8192,128]{1,0:T(8,128)}, f32[128,128]{1,0:T(8,128)}) custom-call(bf16[4096,256]{1,0:T(8,128)(2,1)S(1)} %get-tuple-element.7.hot, bf16[256,256]{1,0:T(8,128)(2,1)S(1)} %bitcast.7, f32[128,128]{1,0:T(8,128)S(1)} %get-tuple-element.9.left), custom_call_target="tpu_custom_call" | custom-call | tf_op jit(solution)/shard_map/dirty/pallas_call | solution.py:614

commit v5 on v4

--- a/solution.py
+++ b/solution.py
@@ -526,7 +526,7 @@
     cells = held.shape[1]
     kept = pltpu.make_async_copy(left, residual, sems.at[1])
     kept.start()
-    first, count = 0, tiles // 64
+    first, count = 0, tiles // 32
     while first < tiles:
         out = lax.dot_general(hot[first : first + count, :], terms[...], NN, preferred_element_type=jnp.float32)
         for c in range(2):
@@ -534,7 +534,7 @@
         at = pl.ds(2 * first, 2 * count)
         pltpu.make_async_copy(held.at[at], dirty.at[at], sems.at[0]).start()
         first += count
-        count = min(tiles - first, first, tiles // 16)
+        count = min(tiles - first, first, tiles // 32)
     pltpu.make_async_copy(held, dirty, sems.at[0]).wait()
     kept.wait()
 

time: 26.8 us -> 26.8 us (level)
  no operation moved by 1% of the time
where the time goes in v5:
time: 26.8 us; the launch traced here: 26.6 us
  Pallas kernels  26 us (97%)
  between operations  0.64 us (2%)
    pallas_call x1, Pallas kernels, on_device(): pl.pallas_call(functools.partial(predict_kernel, group, beams, tiles_dev)...  23.8 us
    pallas_call x1, Pallas kernels, on_device(): pl.pallas_call(dirty_kernel, out_shape=(jax.ShapeDtypeStruct((tiles_dev *...  2.2 us

profile of v5, /device:TPU:0, one launch (start us, length us, event | category | flops | bytes accessed | tf_op | source)
XLA Modules:
  0.0 26.6 jit_solution(1676584342467654059)
XLA Ops:
  0.6 23.8 %predict.1 = (f32[128,128]{1,0:T(8,128)S(1)}, bf16[4,64,256]{2,1,0:T(8,128)(2,1)S(1)}, bf16[4096,256]{1,0:T(8,128)(2,1)S(1)}) custom-call(bf16[512,1024]{1,0:T(8,128)(2,1)} %sky.1, bf16[512,2048]{1,0:T(8,128)(2,1)} %bitcast.8, bf16[64,128,128]{2,1,0:T(8,128)(2,1)} %bitcast.9, f32[128,128]{1,0:T(8,128)} %bitcast.10, s32[1,64]{1,0:T(1,128)} %bitcast.11, ...), custom_call_target="tpu_custom_call" | custom-call | tf_op jit(solution)/shard_map/predict/pallas_call | solution.py:562
  24.4 2.2 %dirty.1 = (f32[8192,128]{1,0:T(8,128)}, f32[128,128]{1,0:T(8,128)}) custom-call(bf16[4096,256]{1,0:T(8,128)(2,1)S(1)} %get-tuple-element.7.hot, bf16[256,256]{1,0:T(8,128)(2,1)S(1)} %bitcast.7, f32[128,128]{1,0:T(8,128)S(1)} %get-tuple-element.9.left), custom_call_target="tpu_custom_call" | custom-call | tf_op jit(solution)/shard_map/dirty/pallas_call | solution.py:614
